TPU v7x, 32 devices: a whole 2x2x4 slice. The times are simulated.
32 devices in a mesh: elem: 4 (over y, x), pulse: 8 (over z, core).
Axes of the slice: x: 2, y: 2, z: 4, core: 2. Of those that a mesh axis runs over, the one named last changes fastest.
Arguments:
- echoes: bfloat16 [2, 2048, 256, 256], P(None, 'elem', 'pulse'), may hold values from -6 to 6
- keep_mask: int32 [256, 8], P('pulse'), may hold values from 0 to 1, as said below
- steer_index: int32 [512], replicated, may hold values from 0 to 1023
- element_position: float32 [2048], replicated, may hold values from 0 to 1024
- element_gain: float32 [2, 2048], replicated, may hold values from -4 to 4
- steer_sines: float32 [1024], replicated, may hold values from -1 to 1
Outputs:
- doppler_power: float32 [512, 256, 256], P('pulse', None, 'elem')
Inputs may be any that keep to these rules, and one draw needn't show every extreme that they name: `keep_mask`: in each masking block, each aligned run of 32 pulses keeps at most 24 pulses, and at least one; in every masking block some run keeps exactly 24.
All inputs are finite; a program needn't handle non-finite values.
Results may differ from a plain program's by a relative error of at most 0.005.
Values may be sent and summed in bfloat16 or wider, within the bound.
No kernel may reach another device: no remote copies, remote signals or barrier semaphores. Data moves between devices by JAX's collectives and lax.ppermute only.
A program may use at most 128 MiB of HBM per device.

v0:
```python
import functools
import math

import jax
import jax.numpy as jnp
import numpy as np
from jax import lax
from jax.experimental import pallas as pl
from jax.experimental.pallas import tpu as pltpu
from jax.sharding import PartitionSpec as P


E = 2048
P_SIZE = 256
LANES = 128
TILE = 16
READS = 2
VMEM = 60 * 1024 * 1024
SHARES = (3, 3, 3, 3)


def tables(count):
    index = jnp.arange(count, dtype=jnp.int32)
    angle = 2.0 * math.pi * (index[:, None] * index[None, :] % count).astype(jnp.float32) / count
    taper = 0.54 - 0.46 * jnp.cos(2.0 * math.pi * index.astype(jnp.float32) / (count - 1))
    taper = taper / math.sqrt(count)
    cos_table = jnp.cos(angle) * taper[None, :]
    sin_table = jnp.sin(angle) * taper[None, :]
    upper = jnp.concatenate((cos_table, sin_table), axis=1)
    lower = jnp.concatenate((-sin_table, cos_table), axis=1)
    transform = jnp.concatenate((upper, lower), axis=0)
    high = transform.astype(jnp.bfloat16)
    low = (transform - high.astype(jnp.float32)).astype(jnp.bfloat16)
    return (high, low)


def cos_sin(phase):
    turns = jnp.floor(phase * (2.0 / math.pi) + 0.5)
    rest = phase - turns * 1.5703125
    rest = rest - turns * 4.837512969970703e-4
    rest = rest - turns * 7.54978995489188e-8
    square = rest * rest
    sine = ((-1.9515295891e-4 * square + 8.3321608736e-3) * square - 1.6666654611e-1) * square * rest + rest
    cosine = (2.443315711809948e-5 * square - 1.388731625493765e-3) * square + 4.166664568298827e-2
    cosine = cosine * square * square - 0.5 * square + 1.0
    quadrant = turns.astype(jnp.int32)
    odd = (quadrant & 1) == 1
    real = jnp.where(odd, sine, cosine)
    imag = jnp.where(odd, cosine, sine)
    real = jnp.where(((quadrant + 1) & 2) == 2, -real, real)
    imag = jnp.where((quadrant & 2) == 2, -imag, imag)
    return (real, imag)


def weight_kernel(me_ref, sine_ref, position_ref, gain_ref, out_ref):
    phase = (2.0 * math.pi * position_ref[...]) * sine_ref[...]
    cosine, sine = cos_sin(phase)
    factor = 1.0 / math.sqrt(E)
    first, second = gain_ref[0:1, :], gain_ref[1:2, :]
    real = ((first * cosine + second * sine) * factor).astype(jnp.bfloat16)
    imag = (second * cosine - first * sine) * factor
    elems = real.shape[1]
    out_ref[:, :elems] = real
    out_ref[:, elems:] = imag.astype(jnp.bfloat16)


def local_weight(me, position, gain, sines, elems):
    beams = sines.shape[0]
    step = min(beams, 128)
    return pl.pallas_call(
        weight_kernel,
        out_shape=jax.ShapeDtypeStruct((beams, 2 * elems), jnp.bfloat16),
        grid_spec=pltpu.PrefetchScalarGridSpec(
            num_scalar_prefetch=1,
            grid=(beams // step,),
            in_specs=[
                pl.BlockSpec((step, 1), lambda i, me: (i, 0)),
                pl.BlockSpec((1, elems), lambda i, me: (0, me[0])),
                pl.BlockSpec((2, elems), lambda i, me: (0, me[0])),
            ],
            out_specs=pl.BlockSpec((step, 2 * elems), lambda i, me: (i, 0)),
        ),
        compiler_params=pltpu.CompilerParams(vmem_limit_bytes=VMEM // 4),
        cost_estimate=pl.CostEstimate(
            flops=40 * beams * elems, bytes_accessed=8 * beams * elems, transcendentals=0
        ),
        name="weights",
    )(me, sines, position, gain)


def slot_sources(mask, slots):
    length = mask.shape[-2]
    zeroed = 1 - mask
    index = jnp.arange(length, dtype=jnp.int32)
    earlier = (index[:, None] > index[None, :]).astype(jnp.int32)
    before = jnp.sum(earlier[:, :, None] * zeroed[..., None, :, :], axis=-2)
    out = (zeroed == 1) & (before < length - slots)
    rank = index[:, None] - jnp.minimum(before, length - slots)
    ids = jnp.arange(slots, dtype=jnp.int32)
    hit = (rank[..., None, :, :] == ids[:, None, None]) & jnp.logical_not(out)[..., None, :, :]
    return hit


def swap_rows(outer, inner):
    row = np.arange(outer * inner)
    return ((row % outer) * inner + row // outer)[:, None] == row[None, :]


def gather_kernel(first, count, offset, per_block, src_ref, swap_ref, *refs):
    xs, out_ref, turned = refs[:-2], refs[-2], refs[-1]
    depth, pulses, all_cells = xs[0].shape[1:]
    elems = READS * depth
    groups = out_ref.shape[1]
    cells = all_cells // groups
    rows = swap_ref.shape[0]
    estep = rows // pulses
    low = lax.broadcasted_iota(jnp.int32, (rows, LANES), 1) < cells
    for start in range(0, elems, estep):
        for at in range(len(xs) // (2 * READS)):
            real, imag = [
                jnp.dot(
                    swap_ref[...],
                    xs[(2 * at + part) * READS + start // depth][
                        0, start % depth : start % depth + estep
                    ].reshape(rows, all_cells),
                    preferred_element_type=jnp.float32,
                )
                for part in range(2)
            ]
            for column in range(all_cells // LANES):
                span = slice(column * LANES, (column + 1) * LANES)
                re, im = real[:, span], imag[:, span]
                even = jnp.where(low, re, pltpu.roll(im, cells, 1))
                odd = jnp.where(low, pltpu.roll(re, cells, 1), im)
                for side, value in enumerate((even, odd)):
                    turned[
                        at * pulses : (at + 1) * pulses, 2 * column + side, start : start + estep, :
                    ] = value.astype(jnp.bfloat16).reshape(pulses, estep, LANES)
    per_group = cells // per_block
    block = lax.broadcasted_iota(jnp.int32, (elems, LANES), 1) % cells // per_block

    def slot(s, carry):
        for group in range(groups):
            place = (first + s) * (groups * per_group) + group * per_group
            value = turned[src_ref[place] - offset, group]
            for piece in range(1, per_group):
                value = jnp.where(block >= piece, turned[src_ref[place + piece] - offset, group], value)
            out_ref[s, group] = value
        return carry

    lax.fori_loop(0, count, slot, 0)


def gather_slots(echoes, sources, first, count, spare, per_block, groups):
    parts, elems, pulses, all_cells = echoes.shape
    chunk = min(elems, 64)
    pstep = min(pulses, TILE)
    estep = TILE * TILE // pstep
    swap = jnp.asarray(swap_rows(estep, pstep), jnp.bfloat16)
    runs = range(first // pstep, (first + count - 1 + spare) // pstep + 1)
    read = echoes.size * len(runs) * pstep // pulses
    return pl.pallas_call(
        functools.partial(gather_kernel, first, count, runs[0] * pstep, per_block),
        out_shape=jax.ShapeDtypeStruct((count, groups, elems, LANES), jnp.bfloat16),
        grid_spec=pltpu.PrefetchScalarGridSpec(
            num_scalar_prefetch=1,
            grid=(elems // chunk,),
            in_specs=[pl.BlockSpec(swap.shape, lambda e, src: (0, 0))]
            + [
                pl.BlockSpec(
                    (1, chunk // READS, pstep, all_cells),
                    functools.partial(
                        lambda part, read, at, e, src: (part, READS * e + read, at, 0), part, read, run
                    ),
                )
                for run in runs
                for part in range(parts)
                for read in range(READS)
            ],
            out_specs=pl.BlockSpec((count, groups, chunk, LANES), lambda e, src: (0, 0, e, 0)),
            scratch_shapes=[pltpu.VMEM((len(runs) * pstep, groups, chunk, LANES), jnp.bfloat16)],
        ),
        compiler_params=pltpu.CompilerParams(vmem_limit_bytes=VMEM - 4 * 1024 * 1024),
        cost_estimate=pl.CostEstimate(
            flops=2 * read * TILE * TILE, bytes_accessed=4 * read, transcendentals=0
        ),
        name="gather_slots",
    )(sources, swap, *([echoes] * (len(runs) * parts * READS)))


def beam_kernel(groups, orders, me_ref, w_ref, *refs):
    xs, outs = refs[: len(orders)], refs[len(orders) :]
    bits = len(orders[0])
    elems = w_ref.shape[1] // 2
    cells = LANES // 2
    sign = jnp.where(lax.broadcasted_iota(jnp.int32, (elems, LANES), 1) < cells, -1.0, 1.0)
    sign = sign.astype(jnp.bfloat16)
    for half, order in enumerate(orders):
        plain, crossed = [], []
        for place in range(groups):
            away = 0
            for at, bit in enumerate(order):
                away |= ((place >> (bits - 1 - at)) & 1) << bit
            value = xs[half][0, me_ref[0] ^ away]
            plain.append(value)
            crossed.append(pltpu.roll(value, cells, 1) * sign)
        both = jnp.concatenate(
            (jnp.concatenate(plain, axis=1), jnp.concatenate(crossed, axis=1)), axis=0
        )
        total = jnp.dot(w_ref[...], both, preferred_element_type=jnp.float32)
        for place in range(groups):
            ref = outs[2 * half + (1 if place >= groups // 2 else 0)]
            value = total[:, place * LANES : (place + 1) * LANES].astype(jnp.bfloat16)
            ref[place % (groups // 2), :, 0] = value.reshape(ref.shape[1], ref.shape[3], LANES)


def form_beams(me, weight, gathered, first, count, orders, owners):
    _, groups, elems, lanes = gathered.shape
    beams = weight.shape[0]
    shape = (groups // 2, owners, count, beams // owners, lanes)
    block = shape[:2] + (1,) + shape[3:]
    starts = [first + half * count for half in range(len(orders))]
    outs = [jax.ShapeDtypeStruct(shape, jnp.bfloat16)] * (2 * len(orders))
    return pl.pallas_call(
        functools.partial(beam_kernel, groups, orders),
        out_shape=outs,
        grid_spec=pltpu.PrefetchScalarGridSpec(
            num_scalar_prefetch=1,
            grid=(count,),
            in_specs=[pl.BlockSpec(weight.shape, lambda i, me: (0, 0))]
            + [
                pl.BlockSpec(
                    (1, groups, elems, lanes), functools.partial(lambda at, i, me: (at + i, 0, 0, 0), at)
                )
                for at in starts
            ],
            out_specs=[pl.BlockSpec(block, lambda i, me: (0, 0, i, 0, 0))] * len(outs),
        ),
        compiler_params=pltpu.CompilerParams(vmem_limit_bytes=VMEM - 4 * 1024 * 1024),
        cost_estimate=pl.CostEstimate(
            flops=4 * len(orders) * count * weight.size * groups * lanes,
            bytes_accessed=2 * weight.size + 8 * len(orders) * count * groups * elems * lanes,
            transcendentals=0,
        ),
        name="form_beams",
    )(me, weight, *([gathered] * len(orders)))


def doppler_kernel(runs, swap_ref, high_ref, low_ref, *refs):
    ins, out_ref, turned, lines = refs[:-3], refs[-3], refs[-2], refs[-1]
    beams = out_ref.shape[0]
    blocks, parts = lines.shape[0], lines.shape[1]
    per_block = out_ref.shape[1] // blocks
    at = 0
    for first in range(0, len(ins), runs):
        slots = ins[first].shape[0]
        rows = jnp.concatenate([ref[...] for ref in ins[first : first + runs]], axis=0)
        for first in range(0, runs * slots, TILE):
            piece = rows[first : first + TILE].reshape(TILE * beams, LANES)
            piece = jnp.dot(swap_ref[...], piece, preferred_element_type=jnp.float32)
            turned[:, at : at + TILE, :] = piece.astype(jnp.bfloat16).reshape(beams, TILE, LANES)
            at += TILE
    for beam in range(beams):
        flipped = turned[beam].T
        for part in range(parts):
            for block in range(blocks):
                row = (part * blocks + block) * per_block
                lines[block, part, beam * per_block : (beam + 1) * per_block, :] = flipped[
                    row : row + per_block
                ]
    for block in range(blocks):
        total = None
        for part in range(parts):
            for table in (high_ref, low_ref):
                term = jnp.dot(
                    lines[block, part], table[block, part], preferred_element_type=jnp.float32
                )
                total = term if total is None else total + term
        count = total.shape[1] // 2
        real, imag = total[:, :count], total[:, count:]
        power = (real * real + imag * imag).reshape(beams, per_block, count)
        out_ref[:, block * per_block : (block + 1) * per_block, :] = power


def doppler(pieces, counts, high, low, per_block):
    blocks, parts, columns, width = high.shape
    runs = len(pieces[0])
    beams = pieces[0][0].shape[1]
    swap = jnp.asarray(swap_rows(TILE, TILE), jnp.bfloat16)
    whole = lambda shape: pl.BlockSpec(shape, lambda i: (0,) * len(shape))
    cells = blocks * per_block
    return pl.pallas_call(
        functools.partial(doppler_kernel, runs),
        out_shape=jax.ShapeDtypeStruct((beams, cells, width // 2), jnp.float32),
        grid=(beams // TILE,),
        in_specs=[whole(swap.shape), whole(high.shape), whole(low.shape)]
        + [
            pl.BlockSpec((slots, TILE, LANES), lambda i: (0, i, 0))
            for slots in counts
            for _ in range(runs)
        ],
        out_specs=pl.BlockSpec((TILE, cells, width // 2), lambda i: (i, 0, 0)),
        scratch_shapes=[
            pltpu.VMEM((TILE, columns, LANES), jnp.bfloat16),
            pltpu.VMEM((blocks, parts, TILE * per_block, columns), jnp.bfloat16),
        ],
        compiler_params=pltpu.CompilerParams(vmem_limit_bytes=VMEM),
        cost_estimate=pl.CostEstimate(
            flops=4 * beams * cells * parts * columns * width,
            bytes_accessed=4 * beams * cells * width,
            transcendentals=0,
        ),
        name="doppler",
    )(swap, high, low, *[piece for chunk in pieces for piece in chunk])


def add(left, right):
    return (left.astype(jnp.float32) + right.astype(jnp.float32)).astype(jnp.bfloat16)


def last_kernel(note, me_ref, *refs):
    owners, count = refs[0].shape[1:3]
    ins, outs = refs[:-owners], refs[-owners:]
    for away in range(owners):
        owner = me_ref[0] ^ away
        for half in range(2):
            total = ins[2 * half][0, owner].astype(jnp.float32)
            total = total + ins[2 * half + 1][0, owner].astype(jnp.float32)
            outs[away][half * count : (half + 1) * count] = total.astype(jnp.bfloat16)
        if note:
            outs[away][2 * count] = ins[4][...]


def last_sum(place, values, note):
    _, owners, count, beams, lanes = values[0].shape
    held = 2 * count + (0 if note is None else 1)
    extra = [] if note is None else [note]
    return pl.pallas_call(
        functools.partial(last_kernel, note is not None),
        out_shape=[jax.ShapeDtypeStruct((held, beams, lanes), jnp.bfloat16)] * owners,
        in_specs=[pl.BlockSpec(memory_space=pltpu.SMEM)]
        + [pl.BlockSpec(memory_space=pltpu.VMEM)] * (4 + len(extra)),
        out_specs=[pl.BlockSpec(memory_space=pltpu.VMEM)] * owners,
        compiler_params=pltpu.CompilerParams(vmem_limit_bytes=VMEM // 4),
        cost_estimate=pl.CostEstimate(
            flops=values[0].size * 2, bytes_accessed=values[0].size * 12, transcendentals=0
        ),
        name="last_sum",
    )(place, *values, *extra)


def per_device(echoes, keep_mask, steer_index, element_position, element_gain, steer_sines):
    groups, owners = lax.axis_size("elem"), lax.axis_size("pulse")
    _, elems, pulses, all_cells = echoes.shape
    blocks_all = keep_mask.shape[1]
    per_block = all_cells // blocks_all
    cells = all_cells // groups
    bits = groups.bit_length() - 1
    slots = (3 * pulses + 3) // 4
    me = lax.axis_index("elem")

    hit = slot_sources(keep_mask, slots)
    sources = jnp.sum(
        jnp.where(hit, jnp.arange(pulses, dtype=jnp.int32)[None, :, None], 0), axis=1
    ).reshape(-1)

    choices = jnp.arange(steer_sines.shape[0], dtype=jnp.int32)
    sines = jnp.sum(
        jnp.where(steer_index[:, None] == choices[None, :], steer_sines[None, :], 0.0),
        axis=1,
        keepdims=True,
    )
    mine = me.astype(jnp.int32).reshape(1)
    place = lax.axis_index("pulse").astype(jnp.int32).reshape(1)
    weight = local_weight(mine, element_position[None, :], element_gain, sines, elems)
    forward = tuple(range(bits))
    orders = (forward, forward[::-1])
    shares = SHARES if sum(SHARES) * 2 == slots else (1,) * (slots // 2)

    def send(value, bit):
        return lax.ppermute(value, "elem", [(i, i ^ (1 << bit)) for i in range(groups)])

    beams = weight.shape[0]
    note = jnp.pad(
        keep_mask.astype(jnp.bfloat16).reshape(-1),
        (0, beams // owners * 2 * cells - keep_mask.size),
    ).reshape(beams // owners, 2 * cells)

    head = gather_slots(echoes, sources, 0, 2 * shares[0], pulses - slots, per_block, groups)
    pieces = []
    summed = []
    first = 0
    for pair, count in enumerate(shares):
        own = weight
        if pair >= 2:
            own = lax.optimization_barrier((weight, summed[pair - 2]))[0]
        if pair == 0:
            outs = form_beams(mine, own, head, 0, count, orders, owners)
        else:
            outs = form_beams(mine, own, tail, first - 2 * shares[0], count, orders, owners)
        first += 2 * count
        if pair == 0:
            where = lax.optimization_barrier((sources, outs[1]))[0]
            tail = gather_slots(
                echoes, where, first, slots - first, pulses - slots, per_block, groups
            )
        states = [(outs[0], outs[1]), (outs[2], outs[3])]
        last = []
        for stage in range(bits):
            for half in range(2):
                keep, away = states[half]
                got = send(away, orders[half][stage])
                if stage == bits - 1:
                    last += [got, keep]
                else:
                    middle = keep.shape[0] // 2
                    states[half] = (
                        add(got[:middle], keep[:middle]),
                        add(got[middle:], keep[middle:]),
                    )
            if stage == 0:
                summed.append(jax.tree.leaves(states)[0])
        final = last_sum(place, last, note if pair == 0 else None)
        arrived = [final[0]]
        for away in range(1, owners):
            arrived.append(
                lax.ppermute(final[away], "pulse", [(i, i ^ away) for i in range(owners)])
            )
        pieces.append(arrived)

    counts = [2 * count for count in shares]
    rows = -(-keep_mask.size // LANES)
    noted = lax.optimization_barrier((pieces[0], pieces[max(len(pieces) - 2, 0)][0]))[0]
    every_mask = jnp.stack([piece[counts[0], :rows].reshape(-1) for piece in noted])
    every_mask = every_mask[:, : keep_mask.size]
    every_mask = every_mask.reshape((owners,) + keep_mask.shape).astype(jnp.int32)
    near = lax.dynamic_slice_in_dim(every_mask, me * (cells // per_block), cells // per_block, 2)
    hits = slot_sources(near, slots)
    hits = hits & (near[:, None] == 1)
    high, low = tables(P_SIZE)
    run_eye = jnp.arange(owners, dtype=jnp.int32)
    order = []
    names = []
    first = 0
    for size in counts:
        part = hits[:, first : first + size]
        order.append(part.reshape(owners * size, pulses, -1))
        names.append(jnp.repeat(run_eye ^ place[0], size))
        first += size
    picks = jnp.concatenate(order, axis=0)
    runs = jnp.concatenate(names)
    onehot = (
        (runs[:, None] == run_eye[None, :])[:, :, None, None] & picks[:, None, :, :]
    ).reshape(picks.shape[0], owners * pulses, -1).astype(jnp.bfloat16)

    def chosen(table):
        halves = table.reshape(2 * P_SIZE, 2, P_SIZE)
        return jnp.einsum(
            "fcp,spk->kcsf", halves, onehot, preferred_element_type=jnp.float32
        ).astype(jnp.bfloat16)

    pieces[0] = noted
    power = doppler(pieces, counts, chosen(high), chosen(low), per_block)
    return jnp.transpose(power, (0, 2, 1))


def solution(mesh):
    placed = (P(None, "elem", "pulse", None), P("pulse", None), P(), P(), P(), P())

    return jax.shard_map(
        per_device, mesh=mesh, in_specs=placed, out_specs=P("pulse", None, "elem"), check_vma=False
    )
```

profile of v0, /device:TPU:0, one launch (start us, length us, event | category | flops | bytes accessed | tf_op | source)
XLA Modules:
  0.0 228.3 jit_solution(15515697962030076352)
XLA Ops:
  5.1 10.6 %gather_slots.2.refs_0_.refs_1_ = bf16[6,4,512,128]{3,2,1,0:T(8,128)(2,1)} custom-call(s32[192]{0:T(256)} %reshape.235.src_ref, bf16[256,256]{1,0:T(8,128)(2,1)} %constant.57.clone.swap_ref, bf16[2,512,32,256]{3,2,1,0:T(8,128)(2,1)} %refs_7_.1, bf16[2,512,32,256]{3,2,1,0:T(8,128)(2,1)} %refs_7_.1, bf16[2,512,32,256]{3,2,1,0:T(8,128)(2,1)} %refs_7_.1, ...), custom_call_target="tpu_custom_call" | custom-call | flops 2147483648 | bytes 16777216 | tf_op jit(solution)/shard_map/gather_slots/pallas_call | solution.py:162
  15.7 3.1 %weights.1.w_ref = bf16[512,1024]{1,0:T(8,128)(2,1)S(1)} custom-call(s32[1]{0:T(128)} %bitcast.2.me_ref, f32[512,1]{1,0:T(8,128)S(1)} %copy.95.sine_ref, f32[1,2048]{1,0:T(1,128)S(1)} %bitcast.37, f32[2,2048]{1,0:T(2,128)S(1)} %copy-done.5), custom_call_target="tpu_custom_call" | custom-call | flops 10485760 | bytes 2097152 | tf_op jit(solution)/shard_map/weights/pallas_call | solution.py:70
  19.8 6.8 %form_beams.4 = (bf16[2,8,3,64,128]{4,3,2,1,0:T(8,128)(2,1)}, bf16[2,8,3,64,128]{4,3,2,1,0:T(8,128)(2,1)}, bf16[2,8,3,64,128]{4,3,2,1,0:T(8,128)(2,1)}, bf16[2,8,3,64,128]{4,3,2,1,0:T(8,128)(2,1)}) custom-call(s32[1]{0:T(128)} %bitcast.2.me_ref, bf16[512,1024]{1,0:T(8,128)(2,1)} %copy-done, bf16[6,4,512,128]{3,2,1,0:T(8,128)(2,1)} %gather_slots.2.refs_0_.refs_1_, ...), custom_call_target="tpu_custom_call" | custom-call | flops 6442450944 | bytes 13631488 | tf_op jit(solution)/shard_map/form_beams/pallas_call | solution.py:224
  26.5 3.0 %collective-permute-start = (bf16[2,8,3,64,128]{4,3,2,1,0:T(8,128)(2,1)}, bf16[2,8,3,64,128]{4,3,2,1,0:T(8,128)(2,1)}, u32[]{:S(2)}, u32[]{:S(2)}) collective-permute-start(bf16[2,8,3,64,128]{4,3,2,1,0:T(8,128)(2,1)} %get-tuple-element.64), channel_id=1, source_target_pairs={{0,8},{8,0},{16,24},{24,16},{1,9},{9,1},{17,25},{25,17},{2,10},{10... | collective-permute-start | bytes 2359304 | tf_op jit(solution)/shard_map/ppermute | solution.py:381
  31.0 16.0 %gather_slots.3.refs_0_.refs_1_ = bf16[18,4,512,128]{3,2,1,0:T(8,128)(2,1)} custom-call(s32[192]{0:T(256)} %reshape.235.src_ref, bf16[256,256]{1,0:T(8,128)(2,1)} %constant.57.clone.swap_ref, bf16[2,512,32,256]{3,2,1,0:T(8,128)(2,1)} %refs_7_.1, bf16[2,512,32,256]{3,2,1,0:T(8,128)(2,1)} %refs_7_.1, bf16[2,512,32,256]{3,2,1,0:T(8,128)(2,1)} %refs_7_.1, ...), custom_call_target="tpu_custom_call" | custom-call | flops 4294967296 | bytes 33554432 | tf_op jit(solution)/shard_map/gather_slots/pallas_call | solution.py:162
  47.0 6.7 %form_beams.6 = (bf16[2,8,3,64,128]{4,3,2,1,0:T(8,128)(2,1)}, bf16[2,8,3,64,128]{4,3,2,1,0:T(8,128)(2,1)}, bf16[2,8,3,64,128]{4,3,2,1,0:T(8,128)(2,1)}, bf16[2,8,3,64,128]{4,3,2,1,0:T(8,128)(2,1)}) custom-call(s32[1]{0:T(128)} %bitcast.2.me_ref, bf16[512,1024]{1,0:T(8,128)(2,1)} %copy-done, bf16[18,4,512,128]{3,2,1,0:T(8,128)(2,1)} %gather_slots.3.refs_0_.refs_1_, ...), custom_call_target="tpu_custom_call" | custom-call | flops 6442450944 | bytes 13631488 | tf_op jit(solution)/shard_map/form_beams/pallas_call | solution.py:224
  62.1 6.8 %form_beams.5 = (bf16[2,8,3,64,128]{4,3,2,1,0:T(8,128)(2,1)}, bf16[2,8,3,64,128]{4,3,2,1,0:T(8,128)(2,1)}, bf16[2,8,3,64,128]{4,3,2,1,0:T(8,128)(2,1)}, bf16[2,8,3,64,128]{4,3,2,1,0:T(8,128)(2,1)}) custom-call(s32[1]{0:T(128)} %bitcast.2.me_ref, bf16[512,1024]{1,0:T(8,128)(2,1)} %copy-done, bf16[18,4,512,128]{3,2,1,0:T(8,128)(2,1)} %gather_slots.3.refs_0_.refs_1_, ...), custom_call_target="tpu_custom_call" | custom-call | flops 6442450944 | bytes 13631488 | tf_op jit(solution)/shard_map/form_beams/pallas_call | solution.py:224
  69.4 5.1 %collective-permute-done.15 = bf16[2,8,3,64,128]{4,3,2,1,0:T(8,128)(2,1)} collective-permute-done((bf16[2,8,3,64,128]{4,3,2,1,0:T(8,128)(2,1)}, bf16[2,8,3,64,128]{4,3,2,1,0:T(8,128)(2,1)}, u32[]{:S(2)}, u32[]{:S(2)}) %collective-permute-start.15) | collective-permute-done | bytes 786464 | tf_op jit(solution)/shard_map/ppermute | solution.py:381
  77.2 6.7 %form_beams.7 = (bf16[2,8,3,64,128]{4,3,2,1,0:T(8,128)(2,1)}, bf16[2,8,3,64,128]{4,3,2,1,0:T(8,128)(2,1)}, bf16[2,8,3,64,128]{4,3,2,1,0:T(8,128)(2,1)}, bf16[2,8,3,64,128]{4,3,2,1,0:T(8,128)(2,1)}) custom-call(s32[1]{0:T(128)} %bitcast.2.me_ref, bf16[512,1024]{1,0:T(8,128)(2,1)} %copy-done, bf16[18,4,512,128]{3,2,1,0:T(8,128)(2,1)} %gather_slots.3.refs_0_.refs_1_, ...), custom_call_target="tpu_custom_call" | custom-call | flops 6442450944 | bytes 13631488 | tf_op jit(solution)/shard_map/form_beams/pallas_call | solution.py:224
  86.5 11.5 %collective-permute-done.11 = bf16[2,8,3,64,128]{4,3,2,1,0:T(8,128)(2,1)S(1)} collective-permute-done((bf16[2,8,3,64,128]{4,3,2,1,0:T(8,128)(2,1)}, bf16[2,8,3,64,128]{4,3,2,1,0:T(8,128)(2,1)S(1)}, u32[]{:S(2)}, u32[]{:S(2)}) %collective-permute-start.11) | collective-permute-done | bytes 786464 | tf_op jit(solution)/shard_map/ppermute | solution.py:381
  104.9 3.7 %collective-permute-done.16.refs_0_ = bf16[1,8,3,64,128]{4,3,2,1,0:T(8,128)(2,1)S(1)} collective-permute-done((bf16[1,8,3,64,128]{4,3,2,1,0:T(8,128)(2,1)}, bf16[1,8,3,64,128]{4,3,2,1,0:T(8,128)(2,1)S(1)}, u32[]{:S(2)}, u32[]{:S(2)}) %collective-permute-start.16) | collective-permute-done | bytes 393248 | tf_op jit(solution)/shard_map/ppermute | solution.py:381
  115.9 11.3 %collective-permute-done.18.refs_2_ = bf16[1,8,3,64,128]{4,3,2,1,0:T(8,128)(2,1)} collective-permute-done((bf16[1,8,3,64,128]{4,3,2,1,0:T(8,128)(2,1)}, bf16[1,8,3,64,128]{4,3,2,1,0:T(8,128)(2,1)}, u32[]{:S(2)}, u32[]{:S(2)}) %collective-permute-start.18) | collective-permute-done | bytes 393248 | tf_op jit(solution)/shard_map/ppermute | solution.py:381
  135.6 2.6 %collective-permute-start.7 = (bf16[7,64,128]{2,1,0:T(8,128)(2,1)S(1)}, bf16[7,64,128]{2,1,0:T(8,128)(2,1)S(1)}, u32[]{:S(2)}, u32[]{:S(2)}) collective-permute-start(bf16[7,64,128]{2,1,0:T(8,128)(2,1)S(1)} %get-tuple-element.72), channel_id=1, source_target_pairs={{0,4},{1,5},{2,6},{3,7},{4,0},{5,1},{6,2},{7,3},{8,12},{9,13},{10,... | collective-permute-start | bytes 344072 | tf_op jit(solution)/shard_map/ppermute | solution.py:427
  138.2 2.9 %collective-permute-start.9 = (bf16[7,64,128]{2,1,0:T(8,128)(2,1)S(1)}, bf16[7,64,128]{2,1,0:T(8,128)(2,1)S(1)}, u32[]{:S(2)}, u32[]{:S(2)}) collective-permute-start(bf16[7,64,128]{2,1,0:T(8,128)(2,1)S(1)} %get-tuple-element.74), channel_id=1, source_target_pairs={{0,6},{1,7},{2,4},{3,5},{4,2},{5,3},{6,0},{7,1},{8,14},{9,15},{10,... | collective-permute-start | bytes 344072 | tf_op jit(solution)/shard_map/ppermute | solution.py:427
  145.2 6.6 %collective-permute-start.20 = (bf16[6,64,128]{2,1,0:T(8,128)(2,1)}, bf16[6,64,128]{2,1,0:T(8,128)(2,1)}, u32[]{:S(2)}, u32[]{:S(2)}) collective-permute-start(bf16[6,64,128]{2,1,0:T(8,128)(2,1)} %get-tuple-element.97), channel_id=1, source_target_pairs={{0,2},{1,3},{2,0},{3,1},{4,6},{5,7},{6,4},{7,5},{8,10},{9,11},{10,... | collective-permute-start | bytes 294920 | tf_op jit(solution)/shard_map/ppermute | solution.py:427
  160.3 6.7 %collective-permute-start.22 = (bf16[6,64,128]{2,1,0:T(8,128)(2,1)}, bf16[6,64,128]{2,1,0:T(8,128)(2,1)}, u32[]{:S(2)}, u32[]{:S(2)}) collective-permute-start(bf16[6,64,128]{2,1,0:T(8,128)(2,1)} %copy-done.11), channel_id=1, source_target_pairs={{0,4},{1,5},{2,6},{3,7},{4,0},{5,1},{6,2},{7,3},{8,12},{9,13},{10,... | collective-permute-start | bytes 294920 | tf_op jit(solution)/shard_map/ppermute | solution.py:427
  171.4 3.8 %collective-permute-start.25 = (bf16[6,64,128]{2,1,0:T(8,128)(2,1)S(1)}, bf16[6,64,128]{2,1,0:T(8,128)(2,1)S(1)}, u32[]{:S(2)}, u32[]{:S(2)}) collective-permute-start(bf16[6,64,128]{2,1,0:T(8,128)(2,1)S(1)} %get-tuple-element.102), channel_id=1, source_target_pairs={{0,7},{1,6},{2,5},{3,4},{4,3},{5,2},{6,1},{7,0},{8,15},{9,14},{10,... | collective-permute-start | bytes 294920 | tf_op jit(solution)/shard_map/ppermute | solution.py:427
  175.2 3.9 %collective-permute-done.22.refs_12_ = bf16[6,64,128]{2,1,0:T(8,128)(2,1)} collective-permute-done((bf16[6,64,128]{2,1,0:T(8,128)(2,1)}, bf16[6,64,128]{2,1,0:T(8,128)(2,1)}, u32[]{:S(2)}, u32[]{:S(2)}) %collective-permute-start.22) | collective-permute-done | bytes 98336 | tf_op jit(solution)/shard_map/ppermute | solution.py:427
  180.6 2.9 %collective-permute-start.29 = (bf16[6,64,128]{2,1,0:T(8,128)(2,1)S(1)}, bf16[6,64,128]{2,1,0:T(8,128)(2,1)S(1)}, u32[]{:S(2)}, u32[]{:S(2)}) collective-permute-start(bf16[6,64,128]{2,1,0:T(8,128)(2,1)S(1)} %get-tuple-element.106), channel_id=1, source_target_pairs={{0,4},{1,5},{2,6},{3,7},{4,0},{5,1},{6,2},{7,3},{8,12},{9,13},{10,... | collective-permute-start | bytes 294920 | tf_op jit(solution)/shard_map/ppermute | solution.py:427
  185.3 2.6 %collective-permute-start.31 = (bf16[6,64,128]{2,1,0:T(8,128)(2,1)S(1)}, bf16[6,64,128]{2,1,0:T(8,128)(2,1)S(1)}, u32[]{:S(2)}, u32[]{:S(2)}) collective-permute-start(bf16[6,64,128]{2,1,0:T(8,128)(2,1)S(1)} %get-tuple-element.108), channel_id=1, source_target_pairs={{0,6},{1,7},{2,4},{3,5},{4,2},{5,3},{6,0},{7,1},{8,14},{9,15},{10,... | collective-permute-start | bytes 294920 | tf_op jit(solution)/shard_map/ppermute | solution.py:427
  189.2 6.5 %collective-permute-done.29.refs_20_ = bf16[6,64,128]{2,1,0:T(8,128)(2,1)S(1)} collective-permute-done((bf16[6,64,128]{2,1,0:T(8,128)(2,1)S(1)}, bf16[6,64,128]{2,1,0:T(8,128)(2,1)S(1)}, u32[]{:S(2)}, u32[]{:S(2)}) %collective-permute-start.29) | collective-permute-done | bytes 98336 | tf_op jit(solution)/shard_map/ppermute | solution.py:427
  206.9 6.8 %collective-permute-done.40.refs_28_ = bf16[6,64,128]{2,1,0:T(8,128)(2,1)S(1)} collective-permute-done((bf16[6,64,128]{2,1,0:T(8,128)(2,1)S(1)}, bf16[6,64,128]{2,1,0:T(8,128)(2,1)S(1)}, u32[]{:S(2)}, u32[]{:S(2)}) %collective-permute-start.40) | collective-permute-done | bytes 98336 | tf_op jit(solution)/shard_map/ppermute | solution.py:427
  213.6 2.9 %collective-permute-done.41.refs_29_ = bf16[6,64,128]{2,1,0:T(8,128)(2,1)S(1)} collective-permute-done((bf16[6,64,128]{2,1,0:T(8,128)(2,1)S(1)}, bf16[6,64,128]{2,1,0:T(8,128)(2,1)S(1)}, u32[]{:S(2)}, u32[]{:S(2)}) %collective-permute-start.41) | collective-permute-done | bytes 98336 | tf_op jit(solution)/shard_map/ppermute | solution.py:427
  217.3 10.9 %doppler.1 = f32[64,64,256]{2,1,0:T(8,128)} custom-call(bf16[256,256]{1,0:T(8,128)(2,1)} %constant.57.clone.swap_ref, bf16[2,2,192,512]{3,2,1,0:T(8,128)(2,1)} %fusion.high_ref, bf16[2,2,192,512]{3,2,1,0:T(8,128)(2,1)} %fusion.1.low_ref, bf16[7,64,128]{2,1,0:T(8,128)(2,1)} %copy-done.7, bf16[7,64,128]{2,1,0:T(8,128)(2,1)} %copy-done.23, ...), custom_call_target="tpu_custom_call" | custom-call | flops 3221225472 | bytes 8388608 | tf_op jit(solution)/shard_map/doppler/pallas_call | solution.py:292
  (241 shorter events, 77.6 us)
Async XLA Ops:
  26.5 30.0 %collective-permute-start = (bf16[2,8,3,64,128]{4,3,2,1,0:T(8,128)(2,1)}, bf16[2,8,3,64,128]{4,3,2,1,0:T(8,128)(2,1)}, u32[]{:S(2)}, u32[]{:S(2)}) collective-permute-start(bf16[2,8,3,64,128]{4,3,2,1,0:T(8,128)(2,1)} %get-tuple-element.64), channel_id=1, source_target_pairs={{0,8},{8,0},{16,24},{24,16},{1,9},{9,1},{17,25},{25,17},{2,10},{10... | collective-permute-start | bytes 2359304 | tf_op jit(solution)/shard_map/ppermute | solution.py:381
  29.5 30.7 %collective-permute-start.2 = (bf16[2,8,3,64,128]{4,3,2,1,0:T(8,128)(2,1)}, bf16[2,8,3,64,128]{4,3,2,1,0:T(8,128)(2,1)S(1)}, u32[]{:S(2)}, u32[]{:S(2)}) collective-permute-start(bf16[2,8,3,64,128]{4,3,2,1,0:T(8,128)(2,1)} %get-tuple-element.66), channel_id=1, source_target_pairs={{0,16},{8,24},{16,0},{24,8},{1,17},{9,25},{17,1},{25,9},{2,18},{10... | collective-permute-start | bytes 2359304 | tf_op jit(solution)/shard_map/ppermute | solution.py:381
  53.7 20.8 %collective-permute-start.15 = (bf16[2,8,3,64,128]{4,3,2,1,0:T(8,128)(2,1)}, bf16[2,8,3,64,128]{4,3,2,1,0:T(8,128)(2,1)}, u32[]{:S(2)}, u32[]{:S(2)}) collective-permute-start(bf16[2,8,3,64,128]{4,3,2,1,0:T(8,128)(2,1)} %get-tuple-element.91), channel_id=1, source_target_pairs={{0,8},{8,0},{16,24},{24,16},{1,9},{9,1},{17,25},{25,17},{2,10},{10... | collective-permute-start | bytes 2359304 | tf_op jit(solution)/shard_map/ppermute | solution.py:381
  54.3 29.6 %collective-permute-start.17 = (bf16[2,8,3,64,128]{4,3,2,1,0:T(8,128)(2,1)}, bf16[2,8,3,64,128]{4,3,2,1,0:T(8,128)(2,1)S(1)}, u32[]{:S(2)}, u32[]{:S(2)}) collective-permute-start(bf16[2,8,3,64,128]{4,3,2,1,0:T(8,128)(2,1)} %get-tuple-element.93), channel_id=1, source_target_pairs={{0,16},{8,24},{16,0},{24,8},{1,17},{9,25},{17,1},{25,9},{2,18},{10... | collective-permute-start | bytes 2359304 | tf_op jit(solution)/shard_map/ppermute | solution.py:381
  58.2 41.4 %collective-permute-start.1 = (bf16[1,8,3,64,128]{4,3,2,1,0:T(8,128)(2,1)S(1)}, bf16[1,8,3,64,128]{4,3,2,1,0:T(8,128)(2,1)S(1)}, u32[]{:S(2)}, u32[]{:S(2)}) collective-permute-start(bf16[1,8,3,64,128]{4,3,2,1,0:T(8,128)(2,1)S(1)} %get-tuple-element.138), channel_id=1, source_target_pairs={{0,16},{8,24},{16,0},{24,8},{1,17},{9,25},{17,1},{25,9},{2,18},{10... | collective-permute-start | bytes 1179656 | tf_op jit(solution)/shard_map/ppermute | solution.py:381
  60.5 42.1 %collective-permute-start.3 = (bf16[1,8,3,64,128]{4,3,2,1,0:T(8,128)(2,1)S(1)}, bf16[1,8,3,64,128]{4,3,2,1,0:T(8,128)(2,1)S(1)}, u32[]{:S(2)}, u32[]{:S(2)}) collective-permute-start(bf16[1,8,3,64,128]{4,3,2,1,0:T(8,128)(2,1)S(1)} %get-tuple-element.136), channel_id=1, source_target_pairs={{0,8},{8,0},{16,24},{24,16},{1,9},{9,1},{17,25},{25,17},{2,10},{10... | collective-permute-start | bytes 1179656 | tf_op jit(solution)/shard_map/ppermute | solution.py:381
  68.8 29.2 %collective-permute-start.11 = (bf16[2,8,3,64,128]{4,3,2,1,0:T(8,128)(2,1)}, bf16[2,8,3,64,128]{4,3,2,1,0:T(8,128)(2,1)S(1)}, u32[]{:S(2)}, u32[]{:S(2)}) collective-permute-start(bf16[2,8,3,64,128]{4,3,2,1,0:T(8,128)(2,1)} %get-tuple-element.78), channel_id=1, source_target_pairs={{0,8},{8,0},{16,24},{24,16},{1,9},{9,1},{17,25},{25,17},{2,10},{10... | collective-permute-start | bytes 2359304 | tf_op jit(solution)/shard_map/ppermute | solution.py:381
  74.5 26.6 %collective-permute-start.13 = (bf16[2,8,3,64,128]{4,3,2,1,0:T(8,128)(2,1)}, bf16[2,8,3,64,128]{4,3,2,1,0:T(8,128)(2,1)S(1)}, u32[]{:S(2)}, u32[]{:S(2)}) collective-permute-start(bf16[2,8,3,64,128]{4,3,2,1,0:T(8,128)(2,1)} %get-tuple-element.80), channel_id=1, source_target_pairs={{0,16},{8,24},{16,0},{24,8},{1,17},{9,25},{17,1},{25,9},{2,18},{10... | collective-permute-start | bytes 2359304 | tf_op jit(solution)/shard_map/ppermute | solution.py:381
  83.9 24.8 %collective-permute-start.16 = (bf16[1,8,3,64,128]{4,3,2,1,0:T(8,128)(2,1)}, bf16[1,8,3,64,128]{4,3,2,1,0:T(8,128)(2,1)S(1)}, u32[]{:S(2)}, u32[]{:S(2)}) collective-permute-start(bf16[1,8,3,64,128]{4,3,2,1,0:T(8,128)(2,1)} %get-tuple-element.130), channel_id=1, source_target_pairs={{0,16},{8,24},{16,0},{24,8},{1,17},{9,25},{17,1},{25,9},{2,18},{10... | collective-permute-start | bytes 1179656 | tf_op jit(solution)/shard_map/ppermute | solution.py:381
  98.0 32.0 %collective-permute-start.33 = (bf16[2,8,3,64,128]{4,3,2,1,0:T(8,128)(2,1)}, bf16[2,8,3,64,128]{4,3,2,1,0:T(8,128)(2,1)}, u32[]{:S(2)}, u32[]{:S(2)}) collective-permute-start(bf16[2,8,3,64,128]{4,3,2,1,0:T(8,128)(2,1)} %get-tuple-element.111), channel_id=1, source_target_pairs={{0,8},{8,0},{16,24},{24,16},{1,9},{9,1},{17,25},{25,17},{2,10},{10... | collective-permute-start | bytes 2359304 | tf_op jit(solution)/shard_map/ppermute | solution.py:381
  99.6 27.5 %collective-permute-start.18 = (bf16[1,8,3,64,128]{4,3,2,1,0:T(8,128)(2,1)}, bf16[1,8,3,64,128]{4,3,2,1,0:T(8,128)(2,1)}, u32[]{:S(2)}, u32[]{:S(2)}) collective-permute-start(bf16[1,8,3,64,128]{4,3,2,1,0:T(8,128)(2,1)} %get-tuple-element.128), channel_id=1, source_target_pairs={{0,8},{8,0},{16,24},{24,16},{1,9},{9,1},{17,25},{25,17},{2,10},{10... | collective-permute-start | bytes 1179656 | tf_op jit(solution)/shard_map/ppermute | solution.py:381
  101.1 37.1 %collective-permute-start.35 = (bf16[2,8,3,64,128]{4,3,2,1,0:T(8,128)(2,1)}, bf16[2,8,3,64,128]{4,3,2,1,0:T(8,128)(2,1)}, u32[]{:S(2)}, u32[]{:S(2)}) collective-permute-start(bf16[2,8,3,64,128]{4,3,2,1,0:T(8,128)(2,1)} %get-tuple-element.113), channel_id=1, source_target_pairs={{0,16},{8,24},{16,0},{24,8},{1,17},{9,25},{17,1},{25,9},{2,18},{10... | collective-permute-start | bytes 2359304 | tf_op jit(solution)/shard_map/ppermute | solution.py:381
  103.4 34.7 %collective-permute-start.12 = (bf16[1,8,3,64,128]{4,3,2,1,0:T(8,128)(2,1)}, bf16[1,8,3,64,128]{4,3,2,1,0:T(8,128)(2,1)S(1)}, u32[]{:S(2)}, u32[]{:S(2)}) collective-permute-start(bf16[1,8,3,64,128]{4,3,2,1,0:T(8,128)(2,1)} %get-tuple-element.134), channel_id=1, source_target_pairs={{0,16},{8,24},{16,0},{24,8},{1,17},{9,25},{17,1},{25,9},{2,18},{10... | collective-permute-start | bytes 1179656 | tf_op jit(solution)/shard_map/ppermute | solution.py:381
  109.4 31.7 %collective-permute-start.14 = (bf16[1,8,3,64,128]{4,3,2,1,0:T(8,128)(2,1)}, bf16[1,8,3,64,128]{4,3,2,1,0:T(8,128)(2,1)S(1)}, u32[]{:S(2)}, u32[]{:S(2)}) collective-permute-start(bf16[1,8,3,64,128]{4,3,2,1,0:T(8,128)(2,1)} %get-tuple-element.132), channel_id=1, source_target_pairs={{0,8},{8,0},{16,24},{24,16},{1,9},{9,1},{17,25},{25,17},{2,10},{10... | collective-permute-start | bytes 1179656 | tf_op jit(solution)/shard_map/ppermute | solution.py:381
  138.2 15.5 %collective-permute-start.8 = (bf16[7,64,128]{2,1,0:T(8,128)(2,1)S(1)}, bf16[7,64,128]{2,1,0:T(8,128)(2,1)S(1)}, u32[]{:S(2)}, u32[]{:S(2)}) collective-permute-start(bf16[7,64,128]{2,1,0:T(8,128)(2,1)S(1)} %get-tuple-element.73), channel_id=1, source_target_pairs={{0,5},{1,4},{2,7},{3,6},{4,1},{5,0},{6,3},{7,2},{8,13},{9,12},{10,... | collective-permute-start | bytes 344072 | tf_op jit(solution)/shard_map/ppermute | solution.py:427
  138.2 15.6 %collective-permute-start.9 = (bf16[7,64,128]{2,1,0:T(8,128)(2,1)S(1)}, bf16[7,64,128]{2,1,0:T(8,128)(2,1)S(1)}, u32[]{:S(2)}, u32[]{:S(2)}) collective-permute-start(bf16[7,64,128]{2,1,0:T(8,128)(2,1)S(1)} %get-tuple-element.74), channel_id=1, source_target_pairs={{0,6},{1,7},{2,4},{3,5},{4,2},{5,3},{6,0},{7,1},{8,14},{9,15},{10,... | collective-permute-start | bytes 344072 | tf_op jit(solution)/shard_map/ppermute | solution.py:427
  144.9 15.4 %collective-permute-start.19 = (bf16[6,64,128]{2,1,0:T(8,128)(2,1)}, bf16[6,64,128]{2,1,0:T(8,128)(2,1)S(1)}, u32[]{:S(2)}, u32[]{:S(2)}) collective-permute-start(bf16[6,64,128]{2,1,0:T(8,128)(2,1)} %get-tuple-element.96), channel_id=1, source_target_pairs={{0,1},{1,0},{2,3},{3,2},{4,5},{5,4},{6,7},{7,6},{8,9},{9,8},{10,11... | collective-permute-start | bytes 294920 | tf_op jit(solution)/shard_map/ppermute | solution.py:427
  145.2 26.2 %collective-permute-start.20 = (bf16[6,64,128]{2,1,0:T(8,128)(2,1)}, bf16[6,64,128]{2,1,0:T(8,128)(2,1)}, u32[]{:S(2)}, u32[]{:S(2)}) collective-permute-start(bf16[6,64,128]{2,1,0:T(8,128)(2,1)} %get-tuple-element.97), channel_id=1, source_target_pairs={{0,2},{1,3},{2,0},{3,1},{4,6},{5,7},{6,4},{7,5},{8,10},{9,11},{10,... | collective-permute-start | bytes 294920 | tf_op jit(solution)/shard_map/ppermute | solution.py:427
  153.6 21.6 %collective-permute-start.21 = (bf16[6,64,128]{2,1,0:T(8,128)(2,1)}, bf16[6,64,128]{2,1,0:T(8,128)(2,1)}, u32[]{:S(2)}, u32[]{:S(2)}) collective-permute-start(bf16[6,64,128]{2,1,0:T(8,128)(2,1)} %get-tuple-element.98), channel_id=1, source_target_pairs={{0,3},{1,2},{2,1},{3,0},{4,7},{5,6},{6,5},{7,4},{8,11},{9,10},{10,... | collective-permute-start | bytes 294920 | tf_op jit(solution)/shard_map/ppermute | solution.py:427
  154.3 14.2 %collective-permute-start.36 = (bf16[1,8,3,64,128]{4,3,2,1,0:T(8,128)(2,1)}, bf16[1,8,3,64,128]{4,3,2,1,0:T(8,128)(2,1)S(1)}, u32[]{:S(2)}, u32[]{:S(2)}) collective-permute-start(bf16[1,8,3,64,128]{4,3,2,1,0:T(8,128)(2,1)} %get-tuple-element.124), channel_id=1, source_target_pairs={{0,8},{8,0},{16,24},{24,16},{1,9},{9,1},{17,25},{25,17},{2,10},{10... | collective-permute-start | bytes 1179656 | tf_op jit(solution)/shard_map/ppermute | solution.py:381
  160.3 18.9 %collective-permute-start.22 = (bf16[6,64,128]{2,1,0:T(8,128)(2,1)}, bf16[6,64,128]{2,1,0:T(8,128)(2,1)}, u32[]{:S(2)}, u32[]{:S(2)}) collective-permute-start(bf16[6,64,128]{2,1,0:T(8,128)(2,1)} %copy-done.11), channel_id=1, source_target_pairs={{0,4},{1,5},{2,6},{3,7},{4,0},{5,1},{6,2},{7,3},{8,12},{9,13},{10,... | collective-permute-start | bytes 294920 | tf_op jit(solution)/shard_map/ppermute | solution.py:427
  180.6 15.2 %collective-permute-start.29 = (bf16[6,64,128]{2,1,0:T(8,128)(2,1)S(1)}, bf16[6,64,128]{2,1,0:T(8,128)(2,1)S(1)}, u32[]{:S(2)}, u32[]{:S(2)}) collective-permute-start(bf16[6,64,128]{2,1,0:T(8,128)(2,1)S(1)} %get-tuple-element.106), channel_id=1, source_target_pairs={{0,4},{1,5},{2,6},{3,7},{4,0},{5,1},{6,2},{7,3},{8,12},{9,13},{10,... | collective-permute-start | bytes 294920 | tf_op jit(solution)/shard_map/ppermute | solution.py:427
  199.0 14.6 %collective-permute-start.40 = (bf16[6,64,128]{2,1,0:T(8,128)(2,1)S(1)}, bf16[6,64,128]{2,1,0:T(8,128)(2,1)S(1)}, u32[]{:S(2)}, u32[]{:S(2)}) collective-permute-start(bf16[6,64,128]{2,1,0:T(8,128)(2,1)S(1)} %get-tuple-element.119), channel_id=1, source_target_pairs={{0,4},{1,5},{2,6},{3,7},{4,0},{5,1},{6,2},{7,3},{8,12},{9,13},{10,... | collective-permute-start | bytes 294920 | tf_op jit(solution)/shard_map/ppermute | solution.py:427
  201.3 15.3 %collective-permute-start.41 = (bf16[6,64,128]{2,1,0:T(8,128)(2,1)S(1)}, bf16[6,64,128]{2,1,0:T(8,128)(2,1)S(1)}, u32[]{:S(2)}, u32[]{:S(2)}) collective-permute-start(bf16[6,64,128]{2,1,0:T(8,128)(2,1)S(1)} %get-tuple-element.120), channel_id=1, source_target_pairs={{0,5},{1,4},{2,7},{3,6},{4,1},{5,0},{6,3},{7,2},{8,13},{9,12},{10,... | collective-permute-start | bytes 294920 | tf_op jit(solution)/shard_map/ppermute | solution.py:427
  (66 other events, 861.9 us)
where the time goes:
time: 231 us; the launch traced here: 228 us
  Pallas kernels  69.8 us (30%)
  starting transfers between devices  60.7 us (26%)
  waiting for transfers between devices  56.6 us (25%)
  other arithmetic  19 us (8%)
  local copies, waits for them, and re-layouts  17.6 us (8%)
  matrix products  3.96 us (2%)
    ppermute x28, starting transfers between devices, per_device(): lax.ppermute(final[away], 'pulse', [(i, i ^ away) for i in range(owners)])  42.8 us
    ppermute x16, waiting for transfers between devices, send(): lax.ppermute(value, 'elem', [(i, i ^ 1 << bit) for i in range(groups)])  31.5 us
    pallas_call x4, Pallas kernels, form_beams(): pl.pallas_call(functools.partial(beam_kernel, groups, orders), out_shape=...  26.9 us
    pallas_call x2, Pallas kernels, gather_slots(): pl.pallas_call(functools.partial(gather_kernel, first, count, runs[0] * p...  26.6 us
    ppermute x28, waiting for transfers between devices, per_device(): lax.ppermute(final[away], 'pulse', [(i, i ^ away) for i in range(owners)])  25 us
    ppermute x16, starting transfers between devices, send(): lax.ppermute(value, 'elem', [(i, i ^ 1 << bit) for i in range(groups)])  17.9 us
    convert_element_type x8, other arithmetic, add(): (left.astype(jnp.float32) + right.astype(jnp.float32)).astype(jnp.bfloat16)  11.6 us
    pallas_call x1, Pallas kernels, doppler(): pl.pallas_call(functools.partial(doppler_kernel, runs), out_shape=jax.Sha...  10.9 us
  transfers between devices with their start and end apart: 44, of which 11 were waited for; matrix products, arithmetic and copies ran while one was open for 13% of the time, Pallas kernels for 17%

commit v1 on v0

--- a/solution.py
+++ b/solution.py
@@ -16,7 +16,7 @@
 TILE = 16
 READS = 2
 VMEM = 60 * 1024 * 1024
-SHARES = (3, 3, 3, 3)
+SHARES = (4, 3, 3, 2)
 
 
 def tables(count):
@@ -249,7 +249,7 @@
 def doppler_kernel(runs, swap_ref, high_ref, low_ref, *refs):
     ins, out_ref, turned, lines = refs[:-3], refs[-3], refs[-2], refs[-1]
     beams = out_ref.shape[0]
-    blocks, parts = lines.shape[0], lines.shape[1]
+    blocks, parts = lines.shape[0], lines.shape[2] // turned.shape[1]
     per_block = out_ref.shape[1] // blocks
     at = 0
     for first in range(0, len(ins), runs):
@@ -260,22 +260,23 @@
             piece = jnp.dot(swap_ref[...], piece, preferred_element_type=jnp.float32)
             turned[:, at : at + TILE, :] = piece.astype(jnp.bfloat16).reshape(beams, TILE, LANES)
             at += TILE
+
+    @pl.when(pl.program_id(0) == 0)
+    def _():
+        turned[:, at:, :] = jnp.zeros((beams, turned.shape[1] - at, LANES), jnp.bfloat16)
+
+    width = turned.shape[1]
     for beam in range(beams):
         flipped = turned[beam].T
         for part in range(parts):
             for block in range(blocks):
                 row = (part * blocks + block) * per_block
-                lines[block, part, beam * per_block : (beam + 1) * per_block, :] = flipped[
-                    row : row + per_block
-                ]
+                lines[
+                    block, beam * per_block : (beam + 1) * per_block, part * width : (part + 1) * width
+                ] = flipped[row : row + per_block]
     for block in range(blocks):
-        total = None
-        for part in range(parts):
-            for table in (high_ref, low_ref):
-                term = jnp.dot(
-                    lines[block, part], table[block, part], preferred_element_type=jnp.float32
-                )
-                total = term if total is None else total + term
+        total = jnp.dot(lines[block], high_ref[block], preferred_element_type=jnp.float32)
+        total = total + jnp.dot(lines[block], low_ref[block], preferred_element_type=jnp.float32)
         count = total.shape[1] // 2
         real, imag = total[:, :count], total[:, count:]
         power = (real * real + imag * imag).reshape(beams, per_block, count)
@@ -293,7 +294,7 @@
         functools.partial(doppler_kernel, runs),
         out_shape=jax.ShapeDtypeStruct((beams, cells, width // 2), jnp.float32),
         grid=(beams // TILE,),
-        in_specs=[whole(swap.shape), whole(high.shape), whole(low.shape)]
+        in_specs=[whole(swap.shape), whole((blocks, parts * columns, width)), whole((blocks, parts * columns, width))]
         + [
             pl.BlockSpec((slots, TILE, LANES), lambda i: (0, i, 0))
             for slots in counts
@@ -302,7 +303,7 @@
         out_specs=pl.BlockSpec((TILE, cells, width // 2), lambda i: (i, 0, 0)),
         scratch_shapes=[
             pltpu.VMEM((TILE, columns, LANES), jnp.bfloat16),
-            pltpu.VMEM((blocks, parts, TILE * per_block, columns), jnp.bfloat16),
+            pltpu.VMEM((blocks, TILE * per_block, parts * columns), jnp.bfloat16),
         ],
         compiler_params=pltpu.CompilerParams(vmem_limit_bytes=VMEM),
         cost_estimate=pl.CostEstimate(
@@ -311,7 +312,12 @@
             transcendentals=0,
         ),
         name="doppler",
-    )(swap, high, low, *[piece for chunk in pieces for piece in chunk])
+    )(
+        swap,
+        high.reshape(blocks, parts * columns, width),
+        low.reshape(blocks, parts * columns, width),
+        *[piece for chunk in pieces for piece in chunk],
+    )
 
 
 def add(left, right):
@@ -347,6 +353,24 @@
         ),
         name="last_sum",
     )(place, *values, *extra)
+
+
+def collect_kernel(*refs):
+    for run, ref in enumerate(refs[:-1]):
+        refs[-1][run] = ref[0]
+
+
+def collect(pieces, slot):
+    lanes = pieces[0].shape[2]
+    return pl.pallas_call(
+        collect_kernel,
+        out_shape=jax.ShapeDtypeStruct((len(pieces), TILE, lanes), jnp.bfloat16),
+        grid=(1,),
+        in_specs=[pl.BlockSpec((1, TILE, lanes), lambda i: (slot, 0, 0))] * len(pieces),
+        out_specs=pl.BlockSpec((len(pieces), TILE, lanes), lambda i: (0, 0, 0)),
+        compiler_params=pltpu.CompilerParams(vmem_limit_bytes=VMEM // 4),
+        name="collect",
+    )(*pieces)
 
 
 def per_device(echoes, keep_mask, steer_index, element_position, element_gain, steer_sines):
@@ -430,8 +454,7 @@
 
     counts = [2 * count for count in shares]
     rows = -(-keep_mask.size // LANES)
-    noted = lax.optimization_barrier((pieces[0], pieces[max(len(pieces) - 2, 0)][0]))[0]
-    every_mask = jnp.stack([piece[counts[0], :rows].reshape(-1) for piece in noted])
+    every_mask = collect(pieces[0], counts[0])[:, :rows].reshape(owners, rows * LANES)
     every_mask = every_mask[:, : keep_mask.size]
     every_mask = every_mask.reshape((owners,) + keep_mask.shape).astype(jnp.int32)
     near = lax.dynamic_slice_in_dim(every_mask, me * (cells // per_block), cells // per_block, 2)
@@ -448,7 +471,9 @@
         names.append(jnp.repeat(run_eye ^ place[0], size))
         first += size
     picks = jnp.concatenate(order, axis=0)
-    runs = jnp.concatenate(names)
+    spare = -picks.shape[0] % 256
+    picks = jnp.pad(picks, ((0, spare), (0, 0), (0, 0)))
+    runs = jnp.pad(jnp.concatenate(names), (0, spare))
     onehot = (
         (runs[:, None] == run_eye[None, :])[:, :, None, None] & picks[:, None, :, :]
     ).reshape(picks.shape[0], owners * pulses, -1).astype(jnp.bfloat16)
@@ -459,7 +484,6 @@
             "fcp,spk->kcsf", halves, onehot, preferred_element_type=jnp.float32
         ).astype(jnp.bfloat16)
 
-    pieces[0] = noted
     power = doppler(pieces, counts, chosen(high), chosen(low), per_block)
     return jnp.transpose(power, (0, 2, 1))
 

time: 231 us -> 245 us (1.061)
  waiting for transfers between devices: 56.6 us -> 78.8 us
  local copies, waits for them, and re-layouts: 17.6 us -> 10 us
  starting transfers between devices: 60.7 us -> 57.6 us
    ppermute x16, waiting for transfers between devices: 31.5 us -> 59.1 us  [send(): lax.ppermute(value, 'elem', [(i, i ^ 1 << bit) for i in range(groups)])]
    ppermute x28, starting transfers between devices: 42.8 us -> 36.1 us  [per_device(): lax.ppermute(final[away], 'pulse', [(i, i ^ away) for i in range(owners)])]
    ppermute x28, waiting for transfers between devices: 25 us -> 19.7 us  [per_device(): lax.ppermute(final[away], 'pulse', [(i, i ^ away) for i in range(owners)])]
    ppermute x16, starting transfers between devices: 17.9 us -> 21.4 us  [send(): lax.ppermute(value, 'elem', [(i, i ^ 1 << bit) for i in range(groups)])]
    slice x8 -> x0, local copies, waits for them, and re-layouts: 3.35 us -> none  [per_device(): piece[counts[0], :rows].reshape(-1)]
    unnamed x92 -> x135, local copies, waits for them, and re-layouts: 5.96 us -> 6.68 us
  transfers between devices with their start and end apart: 44 -> 44, of which waited for: 11 -> 11; matrix products, arithmetic and copies ran while one was open for 13% -> 9% of each run, Pallas kernels for 17% -> 6%
where the time goes in v1:
time: 245 us; the launch traced here: 242 us
  waiting for transfers between devices  78.8 us (32%)
  Pallas kernels  71.6 us (29%)
  starting transfers between devices  57.6 us (24%)
  other arithmetic  20 us (8%)
  local copies, waits for them, and re-layouts  10 us (4%)
  matrix products  2.92 us (1%)
    ppermute x16, waiting for transfers between devices, send(): lax.ppermute(value, 'elem', [(i, i ^ 1 << bit) for i in range(groups)])  59.1 us
    ppermute x28, starting transfers between devices, per_device(): lax.ppermute(final[away], 'pulse', [(i, i ^ away) for i in range(owners)])  36.1 us
    pallas_call x4, Pallas kernels, form_beams(): pl.pallas_call(functools.partial(beam_kernel, groups, orders), out_shape=...  26.7 us
    pallas_call x2, Pallas kernels, gather_slots(): pl.pallas_call(functools.partial(gather_kernel, first, count, runs[0] * p...  26.7 us
    ppermute x16, starting transfers between devices, send(): lax.ppermute(value, 'elem', [(i, i ^ 1 << bit) for i in range(groups)])  21.4 us
    ppermute x28, waiting for transfers between devices, per_device(): lax.ppermute(final[away], 'pulse', [(i, i ^ away) for i in range(owners)])  19.7 us
    convert_element_type x8, other arithmetic, add(): (left.astype(jnp.float32) + right.astype(jnp.float32)).astype(jnp.bfloat16)  13.2 us
    pallas_call x1, Pallas kernels, doppler(): pl.pallas_call(functools.partial(doppler_kernel, runs), out_shape=jax.Sha...  11.5 us
  transfers between devices with their start and end apart: 44, of which 11 were waited for; matrix products, arithmetic and copies ran while one was open for 9% of the time, Pallas kernels for 6%

profile of v1, /device:TPU:0, one launch (start us, length us, event | category | flops | bytes accessed | tf_op | source)
XLA Modules:
  0.0 241.9 jit_solution(15275984883813406395)
XLA Ops:
  4.5 11.0 %gather_slots.2.refs_0_.refs_1_ = bf16[8,4,512,128]{3,2,1,0:T(8,128)(2,1)} custom-call(s32[192]{0:T(256)} %reshape.232.src_ref, bf16[256,256]{1,0:T(8,128)(2,1)} %constant.61.clone.swap_ref, bf16[2,512,32,256]{3,2,1,0:T(8,128)(2,1)} %refs_7_.1, bf16[2,512,32,256]{3,2,1,0:T(8,128)(2,1)} %refs_7_.1, bf16[2,512,32,256]{3,2,1,0:T(8,128)(2,1)} %refs_7_.1, ...), custom_call_target="tpu_custom_call" | custom-call | flops 2147483648 | bytes 16777216 | tf_op jit(solution)/shard_map/gather_slots/pallas_call | solution.py:162
  15.5 3.1 %weights.1.w_ref = bf16[512,1024]{1,0:T(8,128)(2,1)S(1)} custom-call(s32[1]{0:T(128)} %bitcast.2.me_ref, f32[512,1]{1,0:T(8,128)S(1)} %copy.46.sine_ref, f32[1,2048]{1,0:T(1,128)S(1)} %bitcast.38, f32[2,2048]{1,0:T(2,128)S(1)} %copy-done.10), custom_call_target="tpu_custom_call" | custom-call | flops 10485760 | bytes 2097152 | tf_op jit(solution)/shard_map/weights/pallas_call | solution.py:70
  19.6 8.1 %form_beams.4 = (bf16[2,8,4,64,128]{4,3,2,1,0:T(8,128)(2,1)}, bf16[2,8,4,64,128]{4,3,2,1,0:T(8,128)(2,1)}, bf16[2,8,4,64,128]{4,3,2,1,0:T(8,128)(2,1)}, bf16[2,8,4,64,128]{4,3,2,1,0:T(8,128)(2,1)}) custom-call(s32[1]{0:T(128)} %bitcast.2.me_ref, bf16[512,1024]{1,0:T(8,128)(2,1)} %copy-done, bf16[8,4,512,128]{3,2,1,0:T(8,128)(2,1)} %gather_slots.2.refs_0_.refs_1_, ...), custom_call_target="tpu_custom_call" | custom-call | flops 8589934592 | bytes 17825792 | tf_op jit(solution)/shard_map/form_beams/pallas_call | solution.py:224
  27.6 15.6 %gather_slots.3.refs_0_.refs_1_ = bf16[16,4,512,128]{3,2,1,0:T(8,128)(2,1)} custom-call(s32[192]{0:T(256)} %reshape.232.src_ref, bf16[256,256]{1,0:T(8,128)(2,1)} %constant.61.clone.swap_ref, bf16[2,512,32,256]{3,2,1,0:T(8,128)(2,1)} %refs_7_.1, bf16[2,512,32,256]{3,2,1,0:T(8,128)(2,1)} %refs_7_.1, bf16[2,512,32,256]{3,2,1,0:T(8,128)(2,1)} %refs_7_.1, ...), custom_call_target="tpu_custom_call" | custom-call | flops 4294967296 | bytes 33554432 | tf_op jit(solution)/shard_map/gather_slots/pallas_call | solution.py:162
  43.2 6.7 %form_beams.5 = (bf16[2,8,3,64,128]{4,3,2,1,0:T(8,128)(2,1)}, bf16[2,8,3,64,128]{4,3,2,1,0:T(8,128)(2,1)}, bf16[2,8,3,64,128]{4,3,2,1,0:T(8,128)(2,1)}, bf16[2,8,3,64,128]{4,3,2,1,0:T(8,128)(2,1)}) custom-call(s32[1]{0:T(128)} %bitcast.2.me_ref, bf16[512,1024]{1,0:T(8,128)(2,1)} %copy-done, bf16[16,4,512,128]{3,2,1,0:T(8,128)(2,1)} %gather_slots.3.refs_0_.refs_1_, ...), custom_call_target="tpu_custom_call" | custom-call | flops 6442450944 | bytes 13631488 | tf_op jit(solution)/shard_map/form_beams/pallas_call | solution.py:224
  49.9 3.0 %collective-permute-start.11 = (bf16[2,8,3,64,128]{4,3,2,1,0:T(8,128)(2,1)}, bf16[2,8,3,64,128]{4,3,2,1,0:T(8,128)(2,1)S(1)}, u32[]{:S(2)}, u32[]{:S(2)}) collective-permute-start(bf16[2,8,3,64,128]{4,3,2,1,0:T(8,128)(2,1)} %get-tuple-element.69), channel_id=1, source_target_pairs={{0,8},{8,0},{16,24},{24,16},{1,9},{9,1},{17,25},{25,17},{2,10},{10... | collective-permute-start | bytes 2359304 | tf_op jit(solution)/shard_map/ppermute | solution.py:405
  58.2 13.3 %collective-permute-done.11 = bf16[2,8,3,64,128]{4,3,2,1,0:T(8,128)(2,1)S(1)} collective-permute-done((bf16[2,8,3,64,128]{4,3,2,1,0:T(8,128)(2,1)}, bf16[2,8,3,64,128]{4,3,2,1,0:T(8,128)(2,1)S(1)}, u32[]{:S(2)}, u32[]{:S(2)}) %collective-permute-start.11) | collective-permute-done | bytes 786464 | tf_op jit(solution)/shard_map/ppermute | solution.py:405
  72.4 2.4 %add_convert_fusion.10 = (bf16[1,8,3,64,128]{4,3,2,1,0:T(8,128)(2,1)S(1)}, bf16[1,8,3,64,128]{4,3,2,1,0:T(8,128)(2,1)}) fusion(bf16[2,8,3,64,128]{4,3,2,1,0:T(8,128)(2,1)} %copy-done.41, bf16[2,8,3,64,128]{4,3,2,1,0:T(8,128)(2,1)} %get-tuple-element.70), kind=kLoop, calls=%fused_computation.16 | loop fusion | flops 1572864 | bytes 2359296 | tf_op jit(solution)/shard_map/convert_element_type | solution.py:324
  76.9 19.3 %collective-permute-done.13 = bf16[2,8,3,64,128]{4,3,2,1,0:T(8,128)(2,1)} collective-permute-done((bf16[2,8,3,64,128]{4,3,2,1,0:T(8,128)(2,1)}, bf16[2,8,3,64,128]{4,3,2,1,0:T(8,128)(2,1)}, u32[]{:S(2)}, u32[]{:S(2)}) %collective-permute-start.13) | collective-permute-done | bytes 786464 | tf_op jit(solution)/shard_map/ppermute | solution.py:405
  100.3 5.3 %form_beams.7 = (bf16[2,8,2,64,128]{4,3,2,1,0:T(8,128)(2,1)}, bf16[2,8,2,64,128]{4,3,2,1,0:T(8,128)(2,1)}, bf16[2,8,2,64,128]{4,3,2,1,0:T(8,128)(2,1)}, bf16[2,8,2,64,128]{4,3,2,1,0:T(8,128)(2,1)}) custom-call(s32[1]{0:T(128)} %bitcast.2.me_ref, bf16[512,1024]{1,0:T(8,128)(2,1)} %copy-done, bf16[16,4,512,128]{3,2,1,0:T(8,128)(2,1)} %gather_slots.3.refs_0_.refs_1_, ...), custom_call_target="tpu_custom_call" | custom-call | flops 4294967296 | bytes 9437184 | tf_op jit(solution)/shard_map/form_beams/pallas_call | solution.py:224
  108.2 2.5 %add_convert_fusion = (bf16[1,8,4,64,128]{4,3,2,1,0:T(8,128)(2,1)S(1)}, bf16[1,8,4,64,128]{4,3,2,1,0:T(8,128)(2,1)}) fusion(bf16[2,8,4,64,128]{4,3,2,1,0:T(8,128)(2,1)} %collective-permute-done.2, bf16[2,8,4,64,128]{4,3,2,1,0:T(8,128)(2,1)S(1)} %copy-done.37), kind=kLoop, calls=%fused_computation.6 | loop fusion | flops 2097152 | bytes 3145728 | tf_op jit(solution)/shard_map/convert_element_type | solution.py:324
  110.7 7.4 %collective-permute-done.33 = bf16[2,8,2,64,128]{4,3,2,1,0:T(8,128)(2,1)S(1)} collective-permute-done((bf16[2,8,2,64,128]{4,3,2,1,0:T(8,128)(2,1)}, bf16[2,8,2,64,128]{4,3,2,1,0:T(8,128)(2,1)S(1)}, u32[]{:S(2)}, u32[]{:S(2)}) %collective-permute-start.33) | collective-permute-done | bytes 524320 | tf_op jit(solution)/shard_map/ppermute | solution.py:405
  123.6 6.9 %collective-permute-done.1.refs_0_ = bf16[1,8,4,64,128]{4,3,2,1,0:T(8,128)(2,1)S(1)} collective-permute-done((bf16[1,8,4,64,128]{4,3,2,1,0:T(8,128)(2,1)S(1)}, bf16[1,8,4,64,128]{4,3,2,1,0:T(8,128)(2,1)S(1)}, u32[]{:S(2)}, u32[]{:S(2)}) %collective-permute-start.1) | collective-permute-done | bytes 524320 | tf_op jit(solution)/shard_map/ppermute | solution.py:405
  136.0 2.6 %collective-permute-start.7 = (bf16[9,64,128]{2,1,0:T(8,128)(2,1)S(1)}, bf16[9,64,128]{2,1,0:T(8,128)(2,1)S(1)}, u32[]{:S(2)}, u32[]{:S(2)}) collective-permute-start(bf16[9,64,128]{2,1,0:T(8,128)(2,1)S(1)} %get-tuple-element.64), channel_id=1, source_target_pairs={{0,4},{1,5},{2,6},{3,7},{4,0},{5,1},{6,2},{7,3},{8,12},{9,13},{10,... | collective-permute-start | bytes 442376 | tf_op jit(solution)/shard_map/ppermute | solution.py:451
  138.7 3.6 %collective-permute-start.9 = (bf16[9,64,128]{2,1,0:T(8,128)(2,1)S(1)}, bf16[9,64,128]{2,1,0:T(8,128)(2,1)S(1)}, u32[]{:S(2)}, u32[]{:S(2)}) collective-permute-start(bf16[9,64,128]{2,1,0:T(8,128)(2,1)S(1)} %get-tuple-element.66), channel_id=1, source_target_pairs={{0,6},{1,7},{2,4},{3,5},{4,2},{5,3},{6,0},{7,1},{8,14},{9,15},{10,... | collective-permute-start | bytes 442376 | tf_op jit(solution)/shard_map/ppermute | solution.py:451
  142.2 3.2 %collective-permute-done.5.refs_2_ = bf16[9,64,128]{2,1,0:T(8,128)(2,1)S(1)} collective-permute-done((bf16[9,64,128]{2,1,0:T(8,128)(2,1)S(1)}, bf16[9,64,128]{2,1,0:T(8,128)(2,1)S(1)}, u32[]{:S(2)}, u32[]{:S(2)}) %collective-permute-start.5) | collective-permute-done | bytes 147488 | tf_op jit(solution)/shard_map/ppermute | solution.py:451
  145.5 6.7 %form_beams.6 = (bf16[2,8,3,64,128]{4,3,2,1,0:T(8,128)(2,1)}, bf16[2,8,3,64,128]{4,3,2,1,0:T(8,128)(2,1)}, bf16[2,8,3,64,128]{4,3,2,1,0:T(8,128)(2,1)}, bf16[2,8,3,64,128]{4,3,2,1,0:T(8,128)(2,1)}) custom-call(s32[1]{0:T(128)} %bitcast.2.me_ref, bf16[512,1024]{1,0:T(8,128)(2,1)} %copy-done, bf16[16,4,512,128]{3,2,1,0:T(8,128)(2,1)} %gather_slots.3.refs_0_.refs_1_, ...), custom_call_target="tpu_custom_call" | custom-call | flops 6442450944 | bytes 13631488 | tf_op jit(solution)/shard_map/form_beams/pallas_call | solution.py:224
  166.6 11.9 %collective-permute-done.22 = bf16[2,8,3,64,128]{4,3,2,1,0:T(8,128)(2,1)} collective-permute-done((bf16[2,8,3,64,128]{4,3,2,1,0:T(8,128)(2,1)}, bf16[2,8,3,64,128]{4,3,2,1,0:T(8,128)(2,1)}, u32[]{:S(2)}, u32[]{:S(2)}) %collective-permute-start.22) | collective-permute-done | bytes 786464 | tf_op jit(solution)/shard_map/ppermute | solution.py:405
  189.1 6.6 %collective-permute-done.18.refs_12_ = bf16[6,64,128]{2,1,0:T(8,128)(2,1)S(1)} collective-permute-done((bf16[6,64,128]{2,1,0:T(8,128)(2,1)S(1)}, bf16[6,64,128]{2,1,0:T(8,128)(2,1)S(1)}, u32[]{:S(2)}, u32[]{:S(2)}) %collective-permute-start.18) | collective-permute-done | bytes 98336 | tf_op jit(solution)/shard_map/ppermute | solution.py:451
  200.7 2.5 %collective-permute-start.40 = (bf16[4,64,128]{2,1,0:T(8,128)(2,1)S(1)}, bf16[4,64,128]{2,1,0:T(8,128)(2,1)S(1)}, u32[]{:S(2)}, u32[]{:S(2)}) collective-permute-start(bf16[4,64,128]{2,1,0:T(8,128)(2,1)S(1)} %copy-done.30), channel_id=1, source_target_pairs={{0,4},{1,5},{2,6},{3,7},{4,0},{5,1},{6,2},{7,3},{8,12},{9,13},{10,... | collective-permute-start | bytes 196616 | tf_op jit(solution)/shard_map/ppermute | solution.py:451
  211.2 2.4 collective-permute-done.41.refs_29_
  213.5 2.7 %collective-permute-start.29 = (bf16[6,64,128]{2,1,0:T(8,128)(2,1)S(1)}, bf16[6,64,128]{2,1,0:T(8,128)(2,1)S(1)}, u32[]{:S(2)}, u32[]{:S(2)}) collective-permute-start(bf16[6,64,128]{2,1,0:T(8,128)(2,1)S(1)} %get-tuple-element.90), channel_id=1, source_target_pairs={{0,4},{1,5},{2,6},{3,7},{4,0},{5,1},{6,2},{7,3},{8,12},{9,13},{10,... | collective-permute-start | bytes 294920 | tf_op jit(solution)/shard_map/ppermute | solution.py:451
  222.1 6.6 %collective-permute-done.29.refs_20_ = bf16[6,64,128]{2,1,0:T(8,128)(2,1)S(1)} collective-permute-done((bf16[6,64,128]{2,1,0:T(8,128)(2,1)S(1)}, bf16[6,64,128]{2,1,0:T(8,128)(2,1)S(1)}, u32[]{:S(2)}, u32[]{:S(2)}) %collective-permute-start.29) | collective-permute-done | bytes 98336 | tf_op jit(solution)/shard_map/ppermute | solution.py:451
  230.2 11.5 %doppler.1 = f32[64,64,256]{2,1,0:T(8,128)} custom-call(bf16[256,256]{1,0:T(8,128)(2,1)} %constant.61.clone.swap_ref, bf16[2,512,512]{2,1,0:T(8,128)(2,1)} %bitcast.42, bf16[2,512,512]{2,1,0:T(8,128)(2,1)} %bitcast.43, bf16[9,64,128]{2,1,0:T(8,128)(2,1)} %copy-done.1, bf16[9,64,128]{2,1,0:T(8,128)(2,1)} %copy-done.2, bf16[9,64,128]{2,1,0:T(8,128)(2,1)} %copy-done.3, ...), custom_call_target="tpu_custom_call" | custom-call | flops 4294967296 | bytes 8388608 | tf_op jit(solution)/shard_map/doppler/pallas_call | solution.py:293
  (269 shorter events, 76.1 us)
Async XLA Ops:
  49.9 21.6 %collective-permute-start.11 = (bf16[2,8,3,64,128]{4,3,2,1,0:T(8,128)(2,1)}, bf16[2,8,3,64,128]{4,3,2,1,0:T(8,128)(2,1)S(1)}, u32[]{:S(2)}, u32[]{:S(2)}) collective-permute-start(bf16[2,8,3,64,128]{4,3,2,1,0:T(8,128)(2,1)} %get-tuple-element.69), channel_id=1, source_target_pairs={{0,8},{8,0},{16,24},{24,16},{1,9},{9,1},{17,25},{25,17},{2,10},{10... | collective-permute-start | bytes 2359304 | tf_op jit(solution)/shard_map/ppermute | solution.py:405
  52.9 52.8 %collective-permute-start = (bf16[2,8,4,64,128]{4,3,2,1,0:T(8,128)(2,1)}, bf16[2,8,4,64,128]{4,3,2,1,0:T(8,128)(2,1)S(1)}, u32[]{:S(2)}, u32[]{:S(2)}) collective-permute-start(bf16[2,8,4,64,128]{4,3,2,1,0:T(8,128)(2,1)} %get-tuple-element.56), channel_id=1, source_target_pairs={{0,8},{8,0},{16,24},{24,16},{1,9},{9,1},{17,25},{25,17},{2,10},{10... | collective-permute-start | bytes 3145736 | tf_op jit(solution)/shard_map/ppermute | solution.py:405
  53.0 55.1 %collective-permute-start.2 = (bf16[2,8,4,64,128]{4,3,2,1,0:T(8,128)(2,1)}, bf16[2,8,4,64,128]{4,3,2,1,0:T(8,128)(2,1)}, u32[]{:S(2)}, u32[]{:S(2)}) collective-permute-start(bf16[2,8,4,64,128]{4,3,2,1,0:T(8,128)(2,1)} %get-tuple-element.58), channel_id=1, source_target_pairs={{0,16},{8,24},{16,0},{24,8},{1,17},{9,25},{17,1},{25,9},{2,18},{10... | collective-permute-start | bytes 3145736 | tf_op jit(solution)/shard_map/ppermute | solution.py:405
  55.0 41.2 %collective-permute-start.13 = (bf16[2,8,3,64,128]{4,3,2,1,0:T(8,128)(2,1)}, bf16[2,8,3,64,128]{4,3,2,1,0:T(8,128)(2,1)}, u32[]{:S(2)}, u32[]{:S(2)}) collective-permute-start(bf16[2,8,3,64,128]{4,3,2,1,0:T(8,128)(2,1)} %get-tuple-element.71), channel_id=1, source_target_pairs={{0,16},{8,24},{16,0},{24,8},{1,17},{9,25},{17,1},{25,9},{2,18},{10... | collective-permute-start | bytes 2359304 | tf_op jit(solution)/shard_map/ppermute | solution.py:405
  74.9 58.8 %collective-permute-start.12 = (bf16[1,8,3,64,128]{4,3,2,1,0:T(8,128)(2,1)}, bf16[1,8,3,64,128]{4,3,2,1,0:T(8,128)(2,1)}, u32[]{:S(2)}, u32[]{:S(2)}) collective-permute-start(bf16[1,8,3,64,128]{4,3,2,1,0:T(8,128)(2,1)} %get-tuple-element.118), channel_id=1, source_target_pairs={{0,16},{8,24},{16,0},{24,8},{1,17},{9,25},{17,1},{25,9},{2,18},{10... | collective-permute-start | bytes 1179656 | tf_op jit(solution)/shard_map/ppermute | solution.py:405
  98.4 37.4 %collective-permute-start.14 = (bf16[1,8,3,64,128]{4,3,2,1,0:T(8,128)(2,1)}, bf16[1,8,3,64,128]{4,3,2,1,0:T(8,128)(2,1)}, u32[]{:S(2)}, u32[]{:S(2)}) collective-permute-start(bf16[1,8,3,64,128]{4,3,2,1,0:T(8,128)(2,1)} %get-tuple-element.116), channel_id=1, source_target_pairs={{0,8},{8,0},{16,24},{24,16},{1,9},{9,1},{17,25},{25,17},{2,10},{10... | collective-permute-start | bytes 1179656 | tf_op jit(solution)/shard_map/ppermute | solution.py:405
  105.7 15.0 %collective-permute-start.35 = (bf16[2,8,2,64,128]{4,3,2,1,0:T(8,128)(2,1)}, bf16[2,8,2,64,128]{4,3,2,1,0:T(8,128)(2,1)S(1)}, u32[]{:S(2)}, u32[]{:S(2)}) collective-permute-start(bf16[2,8,2,64,128]{4,3,2,1,0:T(8,128)(2,1)} %get-tuple-element.97), channel_id=1, source_target_pairs={{0,16},{8,24},{16,0},{24,8},{1,17},{9,25},{17,1},{25,9},{2,18},{10... | collective-permute-start | bytes 1572872 | tf_op jit(solution)/shard_map/ppermute | solution.py:405
  108.1 22.4 %collective-permute-start.1 = (bf16[1,8,4,64,128]{4,3,2,1,0:T(8,128)(2,1)S(1)}, bf16[1,8,4,64,128]{4,3,2,1,0:T(8,128)(2,1)S(1)}, u32[]{:S(2)}, u32[]{:S(2)}) collective-permute-start(bf16[1,8,4,64,128]{4,3,2,1,0:T(8,128)(2,1)S(1)} %get-tuple-element.110), channel_id=1, source_target_pairs={{0,16},{8,24},{16,0},{24,8},{1,17},{9,25},{17,1},{25,9},{2,18},{10... | collective-permute-start | bytes 1572872 | tf_op jit(solution)/shard_map/ppermute | solution.py:405
  118.1 14.5 %collective-permute-start.3 = (bf16[1,8,4,64,128]{4,3,2,1,0:T(8,128)(2,1)}, bf16[1,8,4,64,128]{4,3,2,1,0:T(8,128)(2,1)S(1)}, u32[]{:S(2)}, u32[]{:S(2)}) collective-permute-start(bf16[1,8,4,64,128]{4,3,2,1,0:T(8,128)(2,1)} %get-tuple-element.108), channel_id=1, source_target_pairs={{0,8},{8,0},{16,24},{24,16},{1,9},{9,1},{17,25},{25,17},{2,10},{10... | collective-permute-start | bytes 1572872 | tf_op jit(solution)/shard_map/ppermute | solution.py:405
  120.7 15.3 %collective-permute-start.34 = (bf16[1,8,2,64,128]{4,3,2,1,0:T(8,128)(2,1)}, bf16[1,8,2,64,128]{4,3,2,1,0:T(8,128)(2,1)}, u32[]{:S(2)}, u32[]{:S(2)}) collective-permute-start(bf16[1,8,2,64,128]{4,3,2,1,0:T(8,128)(2,1)} %get-tuple-element.122), channel_id=1, source_target_pairs={{0,16},{8,24},{16,0},{24,8},{1,17},{9,25},{17,1},{25,9},{2,18},{10... | collective-permute-start | bytes 786440 | tf_op jit(solution)/shard_map/ppermute | solution.py:405
  135.8 22.2 %collective-permute-start.6 = (bf16[9,64,128]{2,1,0:T(8,128)(2,1)S(1)}, bf16[9,64,128]{2,1,0:T(8,128)(2,1)S(1)}, u32[]{:S(2)}, u32[]{:S(2)}) collective-permute-start(bf16[9,64,128]{2,1,0:T(8,128)(2,1)S(1)} %get-tuple-element.63), channel_id=1, source_target_pairs={{0,3},{1,2},{2,1},{3,0},{4,7},{5,6},{6,5},{7,4},{8,11},{9,10},{10,... | collective-permute-start | bytes 442376 | tf_op jit(solution)/shard_map/ppermute | solution.py:451
  136.0 23.1 %collective-permute-start.7 = (bf16[9,64,128]{2,1,0:T(8,128)(2,1)S(1)}, bf16[9,64,128]{2,1,0:T(8,128)(2,1)S(1)}, u32[]{:S(2)}, u32[]{:S(2)}) collective-permute-start(bf16[9,64,128]{2,1,0:T(8,128)(2,1)S(1)} %get-tuple-element.64), channel_id=1, source_target_pairs={{0,4},{1,5},{2,6},{3,7},{4,0},{5,1},{6,2},{7,3},{8,12},{9,13},{10,... | collective-permute-start | bytes 442376 | tf_op jit(solution)/shard_map/ppermute | solution.py:451
  138.6 22.0 %collective-permute-start.8 = (bf16[9,64,128]{2,1,0:T(8,128)(2,1)S(1)}, bf16[9,64,128]{2,1,0:T(8,128)(2,1)S(1)}, u32[]{:S(2)}, u32[]{:S(2)}) collective-permute-start(bf16[9,64,128]{2,1,0:T(8,128)(2,1)S(1)} %get-tuple-element.65), channel_id=1, source_target_pairs={{0,5},{1,4},{2,7},{3,6},{4,1},{5,0},{6,3},{7,2},{8,13},{9,12},{10,... | collective-permute-start | bytes 442376 | tf_op jit(solution)/shard_map/ppermute | solution.py:451
  138.7 22.8 %collective-permute-start.9 = (bf16[9,64,128]{2,1,0:T(8,128)(2,1)S(1)}, bf16[9,64,128]{2,1,0:T(8,128)(2,1)S(1)}, u32[]{:S(2)}, u32[]{:S(2)}) collective-permute-start(bf16[9,64,128]{2,1,0:T(8,128)(2,1)S(1)} %get-tuple-element.66), channel_id=1, source_target_pairs={{0,6},{1,7},{2,4},{3,5},{4,2},{5,3},{6,0},{7,1},{8,14},{9,15},{10,... | collective-permute-start | bytes 442376 | tf_op jit(solution)/shard_map/ppermute | solution.py:451
  145.5 17.9 %collective-permute-start.10 = (bf16[9,64,128]{2,1,0:T(8,128)(2,1)S(1)}, bf16[9,64,128]{2,1,0:T(8,128)(2,1)S(1)}, u32[]{:S(2)}, u32[]{:S(2)}) collective-permute-start(bf16[9,64,128]{2,1,0:T(8,128)(2,1)S(1)} %get-tuple-element.67), channel_id=1, source_target_pairs={{0,7},{1,6},{2,5},{3,4},{4,3},{5,2},{6,1},{7,0},{8,15},{9,14},{10,... | collective-permute-start | bytes 442376 | tf_op jit(solution)/shard_map/ppermute | solution.py:451
  158.0 20.4 %collective-permute-start.22 = (bf16[2,8,3,64,128]{4,3,2,1,0:T(8,128)(2,1)}, bf16[2,8,3,64,128]{4,3,2,1,0:T(8,128)(2,1)}, u32[]{:S(2)}, u32[]{:S(2)}) collective-permute-start(bf16[2,8,3,64,128]{4,3,2,1,0:T(8,128)(2,1)} %get-tuple-element.82), channel_id=1, source_target_pairs={{0,8},{8,0},{16,24},{24,16},{1,9},{9,1},{17,25},{25,17},{2,10},{10... | collective-permute-start | bytes 2359304 | tf_op jit(solution)/shard_map/ppermute | solution.py:405
  159.1 23.2 %collective-permute-start.24 = (bf16[2,8,3,64,128]{4,3,2,1,0:T(8,128)(2,1)}, bf16[2,8,3,64,128]{4,3,2,1,0:T(8,128)(2,1)}, u32[]{:S(2)}, u32[]{:S(2)}) collective-permute-start(bf16[2,8,3,64,128]{4,3,2,1,0:T(8,128)(2,1)} %get-tuple-element.84), channel_id=1, source_target_pairs={{0,16},{8,24},{16,0},{24,8},{1,17},{9,25},{17,1},{25,9},{2,18},{10... | collective-permute-start | bytes 2359304 | tf_op jit(solution)/shard_map/ppermute | solution.py:405
  160.7 24.6 %collective-permute-start.15 = (bf16[6,64,128]{2,1,0:T(8,128)(2,1)}, bf16[6,64,128]{2,1,0:T(8,128)(2,1)}, u32[]{:S(2)}, u32[]{:S(2)}) collective-permute-start(bf16[6,64,128]{2,1,0:T(8,128)(2,1)} %get-tuple-element.74), channel_id=1, source_target_pairs={{0,1},{1,0},{2,3},{3,2},{4,5},{5,4},{6,7},{7,6},{8,9},{9,8},{10,11... | collective-permute-start | bytes 294920 | tf_op jit(solution)/shard_map/ppermute | solution.py:451
  161.5 23.8 %collective-permute-start.16 = (bf16[6,64,128]{2,1,0:T(8,128)(2,1)}, bf16[6,64,128]{2,1,0:T(8,128)(2,1)}, u32[]{:S(2)}, u32[]{:S(2)}) collective-permute-start(bf16[6,64,128]{2,1,0:T(8,128)(2,1)} %get-tuple-element.75), channel_id=1, source_target_pairs={{0,2},{1,3},{2,0},{3,1},{4,6},{5,7},{6,4},{7,5},{8,10},{9,11},{10,... | collective-permute-start | bytes 294920 | tf_op jit(solution)/shard_map/ppermute | solution.py:451
  163.4 24.1 %collective-permute-start.17 = (bf16[6,64,128]{2,1,0:T(8,128)(2,1)}, bf16[6,64,128]{2,1,0:T(8,128)(2,1)}, u32[]{:S(2)}, u32[]{:S(2)}) collective-permute-start(bf16[6,64,128]{2,1,0:T(8,128)(2,1)} %get-tuple-element.76), channel_id=1, source_target_pairs={{0,3},{1,2},{2,1},{3,0},{4,7},{5,6},{6,5},{7,4},{8,11},{9,10},{10,... | collective-permute-start | bytes 294920 | tf_op jit(solution)/shard_map/ppermute | solution.py:451
  180.8 19.9 %collective-permute-start.23 = (bf16[1,8,3,64,128]{4,3,2,1,0:T(8,128)(2,1)}, bf16[1,8,3,64,128]{4,3,2,1,0:T(8,128)(2,1)S(1)}, u32[]{:S(2)}, u32[]{:S(2)}) collective-permute-start(bf16[1,8,3,64,128]{4,3,2,1,0:T(8,128)(2,1)} %get-tuple-element.114), channel_id=1, source_target_pairs={{0,16},{8,24},{16,0},{24,8},{1,17},{9,25},{17,1},{25,9},{2,18},{10... | collective-permute-start | bytes 1179656 | tf_op jit(solution)/shard_map/ppermute | solution.py:405
  184.1 16.6 %collective-permute-start.25 = (bf16[1,8,3,64,128]{4,3,2,1,0:T(8,128)(2,1)S(1)}, bf16[1,8,3,64,128]{4,3,2,1,0:T(8,128)(2,1)S(1)}, u32[]{:S(2)}, u32[]{:S(2)}) collective-permute-start(bf16[1,8,3,64,128]{4,3,2,1,0:T(8,128)(2,1)S(1)} %get-tuple-element.112), channel_id=1, source_target_pairs={{0,8},{8,0},{16,24},{24,16},{1,9},{9,1},{17,25},{25,17},{2,10},{10... | collective-permute-start | bytes 1179656 | tf_op jit(solution)/shard_map/ppermute | solution.py:405
  213.5 15.1 %collective-permute-start.29 = (bf16[6,64,128]{2,1,0:T(8,128)(2,1)S(1)}, bf16[6,64,128]{2,1,0:T(8,128)(2,1)S(1)}, u32[]{:S(2)}, u32[]{:S(2)}) collective-permute-start(bf16[6,64,128]{2,1,0:T(8,128)(2,1)S(1)} %get-tuple-element.90), channel_id=1, source_target_pairs={{0,4},{1,5},{2,6},{3,7},{4,0},{5,1},{6,2},{7,3},{8,12},{9,13},{10,... | collective-permute-start | bytes 294920 | tf_op jit(solution)/shard_map/ppermute | solution.py:451
  216.2 13.2 %collective-permute-start.30 = (bf16[6,64,128]{2,1,0:T(8,128)(2,1)S(1)}, bf16[6,64,128]{2,1,0:T(8,128)(2,1)S(1)}, u32[]{:S(2)}, u32[]{:S(2)}) collective-permute-start(bf16[6,64,128]{2,1,0:T(8,128)(2,1)S(1)} %get-tuple-element.91), channel_id=1, source_target_pairs={{0,5},{1,4},{2,7},{3,6},{4,1},{5,0},{6,3},{7,2},{8,13},{9,12},{10,... | collective-permute-start | bytes 294920 | tf_op jit(solution)/shard_map/ppermute | solution.py:451
  (87 other events, 1050.9 us)

commit v2 on v1

--- a/solution.py
+++ b/solution.py
@@ -246,8 +246,10 @@
     )(me, weight, *([gathered] * len(orders)))
 
 
-def doppler_kernel(runs, swap_ref, high_ref, low_ref, *refs):
+def doppler_kernel(runs, last, prior, swap_ref, high_ref, low_ref, *refs):
     ins, out_ref, turned, lines = refs[:-3], refs[-3], refs[-2], refs[-1]
+    if prior:
+        prior_ref, ins = ins[0], ins[1:]
     beams = out_ref.shape[0]
     blocks, parts = lines.shape[0], lines.shape[2] // turned.shape[1]
     per_block = out_ref.shape[1] // blocks
@@ -261,9 +263,11 @@
             turned[:, at : at + TILE, :] = piece.astype(jnp.bfloat16).reshape(beams, TILE, LANES)
             at += TILE
 
-    @pl.when(pl.program_id(0) == 0)
-    def _():
-        turned[:, at:, :] = jnp.zeros((beams, turned.shape[1] - at, LANES), jnp.bfloat16)
+    if at < turned.shape[1]:
+
+        @pl.when(pl.program_id(0) == 0)
+        def _():
+            turned[:, at:, :] = jnp.zeros((beams, turned.shape[1] - at, LANES), jnp.bfloat16)
 
     width = turned.shape[1]
     for beam in range(beams):
@@ -277,30 +281,39 @@
     for block in range(blocks):
         total = jnp.dot(lines[block], high_ref[block], preferred_element_type=jnp.float32)
         total = total + jnp.dot(lines[block], low_ref[block], preferred_element_type=jnp.float32)
-        count = total.shape[1] // 2
-        real, imag = total[:, :count], total[:, count:]
-        power = (real * real + imag * imag).reshape(beams, per_block, count)
-        out_ref[:, block * per_block : (block + 1) * per_block, :] = power
-
-
-def doppler(pieces, counts, high, low, per_block):
+        cells = slice(block * per_block, (block + 1) * per_block)
+        total = total.reshape(beams, per_block, total.shape[1])
+        if prior:
+            total = total + prior_ref[:, cells, :]
+        if last:
+            count = total.shape[2] // 2
+            real, imag = total[..., :count], total[..., count:]
+            out_ref[:, cells, :] = real * real + imag * imag
+        else:
+            out_ref[:, cells, :] = total
+
+
+def doppler(pieces, counts, high, low, per_block, prior, last):
     blocks, parts, columns, width = high.shape
     runs = len(pieces[0])
     beams = pieces[0][0].shape[1]
     swap = jnp.asarray(swap_rows(TILE, TILE), jnp.bfloat16)
     whole = lambda shape: pl.BlockSpec(shape, lambda i: (0,) * len(shape))
     cells = blocks * per_block
+    bins = width // 2 if last else width
+    held = [] if prior is None else [prior]
     return pl.pallas_call(
-        functools.partial(doppler_kernel, runs),
-        out_shape=jax.ShapeDtypeStruct((beams, cells, width // 2), jnp.float32),
+        functools.partial(doppler_kernel, runs, last, prior is not None),
+        out_shape=jax.ShapeDtypeStruct((beams, cells, bins), jnp.float32),
         grid=(beams // TILE,),
         in_specs=[whole(swap.shape), whole((blocks, parts * columns, width)), whole((blocks, parts * columns, width))]
+        + [pl.BlockSpec((TILE, cells, width), lambda i: (i, 0, 0))] * len(held)
         + [
             pl.BlockSpec((slots, TILE, LANES), lambda i: (0, i, 0))
             for slots in counts
             for _ in range(runs)
         ],
-        out_specs=pl.BlockSpec((TILE, cells, width // 2), lambda i: (i, 0, 0)),
+        out_specs=pl.BlockSpec((TILE, cells, bins), lambda i: (i, 0, 0)),
         scratch_shapes=[
             pltpu.VMEM((TILE, columns, LANES), jnp.bfloat16),
             pltpu.VMEM((blocks, TILE * per_block, parts * columns), jnp.bfloat16),
@@ -316,6 +329,7 @@
         swap,
         high.reshape(blocks, parts * columns, width),
         low.reshape(blocks, parts * columns, width),
+        *held,
         *[piece for chunk in pieces for piece in chunk],
     )
 
@@ -462,29 +476,35 @@
     hits = hits & (near[:, None] == 1)
     high, low = tables(P_SIZE)
     run_eye = jnp.arange(owners, dtype=jnp.int32)
-    order = []
-    names = []
-    first = 0
-    for size in counts:
-        part = hits[:, first : first + size]
-        order.append(part.reshape(owners * size, pulses, -1))
-        names.append(jnp.repeat(run_eye ^ place[0], size))
-        first += size
-    picks = jnp.concatenate(order, axis=0)
-    spare = -picks.shape[0] % 256
-    picks = jnp.pad(picks, ((0, spare), (0, 0), (0, 0)))
-    runs = jnp.pad(jnp.concatenate(names), (0, spare))
-    onehot = (
-        (runs[:, None] == run_eye[None, :])[:, :, None, None] & picks[:, None, :, :]
-    ).reshape(picks.shape[0], owners * pulses, -1).astype(jnp.bfloat16)
-
-    def chosen(table):
-        halves = table.reshape(2 * P_SIZE, 2, P_SIZE)
-        return jnp.einsum(
-            "fcp,spk->kcsf", halves, onehot, preferred_element_type=jnp.float32
-        ).astype(jnp.bfloat16)
-
-    power = doppler(pieces, counts, chosen(high), chosen(low), per_block)
+
+    def chosen(first, last):
+        order, names = [], []
+        for pair in range(first, last):
+            size, at = counts[pair], sum(counts[:pair])
+            order.append(hits[:, at : at + size].reshape(owners * size, pulses, -1))
+            names.append(jnp.repeat(run_eye ^ place[0], size))
+        picks = jnp.concatenate(order, axis=0)
+        spare = -picks.shape[0] % LANES
+        picks = jnp.pad(picks, ((0, spare), (0, 0), (0, 0)))
+        runs = jnp.pad(jnp.concatenate(names), (0, spare))
+        onehot = (
+            (runs[:, None] == run_eye[None, :])[:, :, None, None] & picks[:, None, :, :]
+        ).reshape(picks.shape[0], owners * pulses, -1).astype(jnp.bfloat16)
+        return [
+            jnp.einsum(
+                "fcp,spk->kcsf",
+                table.reshape(2 * P_SIZE, 2, P_SIZE),
+                onehot,
+                preferred_element_type=jnp.float32,
+            ).astype(jnp.bfloat16)
+            for table in (high, low)
+        ]
+
+    pairs = len(counts)
+    partial = doppler(
+        pieces[:-1], counts[:-1], *chosen(0, pairs - 1), per_block, None, False
+    )
+    power = doppler(pieces[-1:], counts[-1:], *chosen(pairs - 1, pairs), per_block, partial, True)
     return jnp.transpose(power, (0, 2, 1))
 
 

time: 245 us -> 249 us (1.016)
  the two profiles are of different devices: /device:TPU:0 before, /device:TPU:13 now
where the time goes in v2:
time: 249 us; the launch traced here: 248 us
  Pallas kernels  79.8 us (32%)
  waiting for transfers between devices  79.7 us (32%)
  starting transfers between devices  52.2 us (21%)
  other arithmetic  18.4 us (7%)
  local copies, waits for them, and re-layouts  11.9 us (5%)
  matrix products  5.2 us (2%)
    ppermute x16, waiting for transfers between devices, send(): lax.ppermute(value, 'elem', [(i, i ^ 1 << bit) for i in range(groups)])  58.6 us
    ppermute x28, starting transfers between devices, per_device(): lax.ppermute(final[away], 'pulse', [(i, i ^ away) for i in range(owners)])  39.7 us
    pallas_call x4, Pallas kernels, form_beams(): pl.pallas_call(functools.partial(beam_kernel, groups, orders), out_shape=...  26.8 us
    pallas_call x2, Pallas kernels, gather_slots(): pl.pallas_call(functools.partial(gather_kernel, first, count, runs[0] * p...  26.6 us
    ppermute x28, waiting for transfers between devices, per_device(): lax.ppermute(final[away], 'pulse', [(i, i ^ away) for i in range(owners)])  21.2 us
    pallas_call x2, Pallas kernels, doppler(): pl.pallas_call(functools.partial(doppler_kernel, runs, last, prior is not...  19.8 us
    ppermute x16, starting transfers between devices, send(): lax.ppermute(value, 'elem', [(i, i ^ 1 << bit) for i in range(groups)])  12.5 us
    convert_element_type x8, other arithmetic, add(): (left.astype(jnp.float32) + right.astype(jnp.float32)).astype(jnp.bfloat16)  10.9 us
  transfers between devices with their start and end apart: 44, of which 10 were waited for; matrix products, arithmetic and copies ran while one was open for 10% of the time, Pallas kernels for 20%

profile of v2, /device:TPU:13, one launch (start us, length us, event | category | flops | bytes accessed | tf_op | source)
XLA Modules:
  0.0 248.2 jit_solution(9794132430281423089)
XLA Ops:
  4.5 11.0 %gather_slots.2.refs_0_.refs_1_ = bf16[8,4,512,128]{3,2,1,0:T(8,128)(2,1)} custom-call(s32[192]{0:T(256)} %reshape.263.src_ref, bf16[256,256]{1,0:T(8,128)(2,1)} %constant.63.clone.swap_ref, bf16[2,512,32,256]{3,2,1,0:T(8,128)(2,1)} %refs_7_.1, bf16[2,512,32,256]{3,2,1,0:T(8,128)(2,1)} %refs_7_.1, bf16[2,512,32,256]{3,2,1,0:T(8,128)(2,1)} %refs_7_.1, ...), custom_call_target="tpu_custom_call" | custom-call | flops 2147483648 | bytes 16777216 | tf_op jit(solution)/shard_map/gather_slots/pallas_call | solution.py:162
  15.5 3.1 %weights.1.w_ref = bf16[512,1024]{1,0:T(8,128)(2,1)S(1)} custom-call(s32[1]{0:T(128)} %bitcast.2.me_ref, f32[512,1]{1,0:T(8,128)S(1)} %copy.51.sine_ref, f32[1,2048]{1,0:T(1,128)S(1)} %bitcast.59, f32[2,2048]{1,0:T(2,128)S(1)} %copy-done.11), custom_call_target="tpu_custom_call" | custom-call | flops 10485760 | bytes 2097152 | tf_op jit(solution)/shard_map/weights/pallas_call | solution.py:70
  19.6 8.1 %form_beams.4 = (bf16[2,8,4,64,128]{4,3,2,1,0:T(8,128)(2,1)}, bf16[2,8,4,64,128]{4,3,2,1,0:T(8,128)(2,1)}, bf16[2,8,4,64,128]{4,3,2,1,0:T(8,128)(2,1)}, bf16[2,8,4,64,128]{4,3,2,1,0:T(8,128)(2,1)}) custom-call(s32[1]{0:T(128)} %bitcast.2.me_ref, bf16[512,1024]{1,0:T(8,128)(2,1)} %copy-done, bf16[8,4,512,128]{3,2,1,0:T(8,128)(2,1)} %gather_slots.2.refs_0_.refs_1_, ...), custom_call_target="tpu_custom_call" | custom-call | flops 8589934592 | bytes 17825792 | tf_op jit(solution)/shard_map/form_beams/pallas_call | solution.py:224
  28.9 15.6 %gather_slots.3.refs_0_.refs_1_ = bf16[16,4,512,128]{3,2,1,0:T(8,128)(2,1)} custom-call(s32[192]{0:T(256)} %reshape.263.src_ref, bf16[256,256]{1,0:T(8,128)(2,1)} %constant.63.clone.swap_ref, bf16[2,512,32,256]{3,2,1,0:T(8,128)(2,1)} %refs_7_.1, bf16[2,512,32,256]{3,2,1,0:T(8,128)(2,1)} %refs_7_.1, bf16[2,512,32,256]{3,2,1,0:T(8,128)(2,1)} %refs_7_.1, ...), custom_call_target="tpu_custom_call" | custom-call | flops 4294967296 | bytes 33554432 | tf_op jit(solution)/shard_map/gather_slots/pallas_call | solution.py:162
  44.5 6.7 %form_beams.5 = (bf16[2,8,3,64,128]{4,3,2,1,0:T(8,128)(2,1)}, bf16[2,8,3,64,128]{4,3,2,1,0:T(8,128)(2,1)}, bf16[2,8,3,64,128]{4,3,2,1,0:T(8,128)(2,1)}, bf16[2,8,3,64,128]{4,3,2,1,0:T(8,128)(2,1)}) custom-call(s32[1]{0:T(128)} %bitcast.2.me_ref, bf16[512,1024]{1,0:T(8,128)(2,1)} %copy-done, bf16[16,4,512,128]{3,2,1,0:T(8,128)(2,1)} %gather_slots.3.refs_0_.refs_1_, ...), custom_call_target="tpu_custom_call" | custom-call | flops 6442450944 | bytes 13631488 | tf_op jit(solution)/shard_map/form_beams/pallas_call | solution.py:224
  56.1 13.6 %collective-permute-done.11 = bf16[2,8,3,64,128]{4,3,2,1,0:T(8,128)(2,1)} collective-permute-done((bf16[2,8,3,64,128]{4,3,2,1,0:T(8,128)(2,1)}, bf16[2,8,3,64,128]{4,3,2,1,0:T(8,128)(2,1)}, u32[]{:S(2)}, u32[]{:S(2)}) %collective-permute-start.11) | collective-permute-done | bytes 786464 | tf_op jit(solution)/shard_map/ppermute | solution.py:419
  72.0 5.3 %form_beams.7 = (bf16[2,8,2,64,128]{4,3,2,1,0:T(8,128)(2,1)}, bf16[2,8,2,64,128]{4,3,2,1,0:T(8,128)(2,1)}, bf16[2,8,2,64,128]{4,3,2,1,0:T(8,128)(2,1)}, bf16[2,8,2,64,128]{4,3,2,1,0:T(8,128)(2,1)}) custom-call(s32[1]{0:T(128)} %bitcast.2.me_ref, bf16[512,1024]{1,0:T(8,128)(2,1)} %copy-done, bf16[16,4,512,128]{3,2,1,0:T(8,128)(2,1)} %gather_slots.3.refs_0_.refs_1_, ...), custom_call_target="tpu_custom_call" | custom-call | flops 4294967296 | bytes 9437184 | tf_op jit(solution)/shard_map/form_beams/pallas_call | solution.py:224
  81.8 10.3 %collective-permute-done.2 = bf16[2,8,4,64,128]{4,3,2,1,0:T(8,128)(2,1)} collective-permute-done((bf16[2,8,4,64,128]{4,3,2,1,0:T(8,128)(2,1)}, bf16[2,8,4,64,128]{4,3,2,1,0:T(8,128)(2,1)}, u32[]{:S(2)}, u32[]{:S(2)}) %collective-permute-start.2) | collective-permute-done | bytes 1048608 | tf_op jit(solution)/shard_map/ppermute | solution.py:419
  94.8 8.4 %collective-permute-done.35 = bf16[2,8,2,64,128]{4,3,2,1,0:T(8,128)(2,1)S(1)} collective-permute-done((bf16[2,8,2,64,128]{4,3,2,1,0:T(8,128)(2,1)}, bf16[2,8,2,64,128]{4,3,2,1,0:T(8,128)(2,1)S(1)}, u32[]{:S(2)}, u32[]{:S(2)}) %collective-permute-start.35) | collective-permute-done | bytes 524320 | tf_op jit(solution)/shard_map/ppermute | solution.py:419
  106.5 16.5 %collective-permute-done.1.refs_0_ = bf16[1,8,4,64,128]{4,3,2,1,0:T(8,128)(2,1)S(1)} collective-permute-done((bf16[1,8,4,64,128]{4,3,2,1,0:T(8,128)(2,1)S(1)}, bf16[1,8,4,64,128]{4,3,2,1,0:T(8,128)(2,1)S(1)}, u32[]{:S(2)}, u32[]{:S(2)}) %collective-permute-start.1) | collective-permute-done | bytes 524320 | tf_op jit(solution)/shard_map/ppermute | solution.py:419
  125.5 3.5 %collective-permute-start.10 = (bf16[9,64,128]{2,1,0:T(8,128)(2,1)S(1)}, bf16[9,64,128]{2,1,0:T(8,128)(2,1)S(1)}, u32[]{:S(2)}, u32[]{:S(2)}) collective-permute-start(bf16[9,64,128]{2,1,0:T(8,128)(2,1)S(1)} %get-tuple-element.67), channel_id=1, source_target_pairs={{0,7},{1,6},{2,5},{3,4},{4,3},{5,2},{6,1},{7,0},{8,15},{9,14},{10,... | collective-permute-start | bytes 442376 | tf_op jit(solution)/shard_map/ppermute | solution.py:465
  132.6 4.3 %collective-permute-done.10.refs_7_ = bf16[9,64,128]{2,1,0:T(8,128)(2,1)S(1)} collective-permute-done((bf16[9,64,128]{2,1,0:T(8,128)(2,1)S(1)}, bf16[9,64,128]{2,1,0:T(8,128)(2,1)S(1)}, u32[]{:S(2)}, u32[]{:S(2)}) %collective-permute-start.10) | collective-permute-done | bytes 147488 | tf_op jit(solution)/shard_map/ppermute | solution.py:465
  137.0 6.7 %form_beams.6 = (bf16[2,8,3,64,128]{4,3,2,1,0:T(8,128)(2,1)}, bf16[2,8,3,64,128]{4,3,2,1,0:T(8,128)(2,1)}, bf16[2,8,3,64,128]{4,3,2,1,0:T(8,128)(2,1)}, bf16[2,8,3,64,128]{4,3,2,1,0:T(8,128)(2,1)}) custom-call(s32[1]{0:T(128)} %bitcast.2.me_ref, bf16[512,1024]{1,0:T(8,128)(2,1)} %copy-done, bf16[16,4,512,128]{3,2,1,0:T(8,128)(2,1)} %gather_slots.3.refs_0_.refs_1_, ...), custom_call_target="tpu_custom_call" | custom-call | flops 6442450944 | bytes 13631488 | tf_op jit(solution)/shard_map/form_beams/pallas_call | solution.py:224
  154.0 2.7 %collective-permute-start.16 = (bf16[6,64,128]{2,1,0:T(8,128)(2,1)}, bf16[6,64,128]{2,1,0:T(8,128)(2,1)}, u32[]{:S(2)}, u32[]{:S(2)}) collective-permute-start(bf16[6,64,128]{2,1,0:T(8,128)(2,1)} %get-tuple-element.75), channel_id=1, source_target_pairs={{0,2},{1,3},{2,0},{3,1},{4,6},{5,7},{6,4},{7,5},{8,10},{9,11},{10,... | collective-permute-start | bytes 294920 | tf_op jit(solution)/shard_map/ppermute | solution.py:465
  158.4 9.7 %collective-permute-done.24 = bf16[2,8,3,64,128]{4,3,2,1,0:T(8,128)(2,1)} collective-permute-done((bf16[2,8,3,64,128]{4,3,2,1,0:T(8,128)(2,1)}, bf16[2,8,3,64,128]{4,3,2,1,0:T(8,128)(2,1)}, u32[]{:S(2)}, u32[]{:S(2)}) %collective-permute-start.24) | collective-permute-done | bytes 786464 | tf_op jit(solution)/shard_map/ppermute | solution.py:419
  176.6 5.3 %collective-permute-start.18 = (bf16[6,64,128]{2,1,0:T(8,128)(2,1)S(1)}, bf16[6,64,128]{2,1,0:T(8,128)(2,1)}, u32[]{:S(2)}, u32[]{:S(2)}) collective-permute-start(bf16[6,64,128]{2,1,0:T(8,128)(2,1)S(1)} %copy-done.21), channel_id=1, source_target_pairs={{0,4},{1,5},{2,6},{3,7},{4,0},{5,1},{6,2},{7,3},{8,12},{9,13},{10,... | collective-permute-start | bytes 294920 | tf_op jit(solution)/shard_map/ppermute | solution.py:465
  181.9 4.0 %collective-permute-start.19 = (bf16[6,64,128]{2,1,0:T(8,128)(2,1)S(1)}, bf16[6,64,128]{2,1,0:T(8,128)(2,1)S(1)}, u32[]{:S(2)}, u32[]{:S(2)}) collective-permute-start(bf16[6,64,128]{2,1,0:T(8,128)(2,1)S(1)} %copy-done.19), channel_id=1, source_target_pairs={{0,5},{1,4},{2,7},{3,6},{4,1},{5,0},{6,3},{7,2},{8,13},{9,12},{10,... | collective-permute-start | bytes 294920 | tf_op jit(solution)/shard_map/ppermute | solution.py:465
  190.5 3.4 %collective-permute-start.38 = (bf16[4,64,128]{2,1,0:T(8,128)(2,1)S(1)}, bf16[4,64,128]{2,1,0:T(8,128)(2,1)S(1)}, u32[]{:S(2)}, u32[]{:S(2)}) collective-permute-start(bf16[4,64,128]{2,1,0:T(8,128)(2,1)S(1)} %copy-done.34), channel_id=1, source_target_pairs={{0,2},{1,3},{2,0},{3,1},{4,6},{5,7},{6,4},{7,5},{8,10},{9,11},{10,... | collective-permute-start | bytes 196616 | tf_op jit(solution)/shard_map/ppermute | solution.py:465
  196.6 3.1 %collective-permute-done.21.refs_15_ = bf16[6,64,128]{2,1,0:T(8,128)(2,1)S(1)} collective-permute-done((bf16[6,64,128]{2,1,0:T(8,128)(2,1)S(1)}, bf16[6,64,128]{2,1,0:T(8,128)(2,1)S(1)}, u32[]{:S(2)}, u32[]{:S(2)}) %collective-permute-start.21) | collective-permute-done | bytes 98336 | tf_op jit(solution)/shard_map/ppermute | solution.py:465
  209.3 5.3 %collective-permute-done.30.refs_21_ = bf16[6,64,128]{2,1,0:T(8,128)(2,1)S(1)} collective-permute-done((bf16[6,64,128]{2,1,0:T(8,128)(2,1)S(1)}, bf16[6,64,128]{2,1,0:T(8,128)(2,1)S(1)}, u32[]{:S(2)}, u32[]{:S(2)}) %collective-permute-start.30) | collective-permute-done | bytes 98336 | tf_op jit(solution)/shard_map/ppermute | solution.py:465
  214.6 3.8 %collective-permute-start.41 = (bf16[4,64,128]{2,1,0:T(8,128)(2,1)S(1)}, bf16[4,64,128]{2,1,0:T(8,128)(2,1)S(1)}, u32[]{:S(2)}, u32[]{:S(2)}) collective-permute-start(bf16[4,64,128]{2,1,0:T(8,128)(2,1)S(1)} %copy-done.28), channel_id=1, source_target_pairs={{0,5},{1,4},{2,7},{3,6},{4,1},{5,0},{6,3},{7,2},{8,13},{9,12},{10,... | collective-permute-start | bytes 196616 | tf_op jit(solution)/shard_map/ppermute | solution.py:465
  219.4 7.6 %collective-permute-done.32.refs_23_ = bf16[6,64,128]{2,1,0:T(8,128)(2,1)S(1)} collective-permute-done((bf16[6,64,128]{2,1,0:T(8,128)(2,1)S(1)}, bf16[6,64,128]{2,1,0:T(8,128)(2,1)S(1)}, u32[]{:S(2)}, u32[]{:S(2)}) %collective-permute-start.32) | collective-permute-done | bytes 98336 | tf_op jit(solution)/shard_map/ppermute | solution.py:465
  227.6 11.5 %doppler.2.refs_0_ = f32[64,64,512]{2,1,0:T(8,128)} custom-call(bf16[256,256]{1,0:T(8,128)(2,1)} %constant.63.clone.swap_ref, bf16[2,512,512]{2,1,0:T(8,128)(2,1)} %bitcast.67, bf16[2,512,512]{2,1,0:T(8,128)(2,1)} %bitcast.66, bf16[9,64,128]{2,1,0:T(8,128)(2,1)} %copy-done.1, bf16[9,64,128]{2,1,0:T(8,128)(2,1)} %copy-done.3, bf16[9,64,128]{2,1,0:T(8,128)(2,1)} %copy-done.4, ...), custom_call_target="tpu_custom_call" | custom-call | flops 4294967296 | bytes 8388608 | tf_op jit(solution)/shard_map/doppler/pallas_call | solution.py:305
  239.9 8.3 %doppler.3 = f32[64,64,256]{2,1,0:T(8,128)} custom-call(bf16[256,256]{1,0:T(8,128)(2,1)} %constant.63.clone.swap_ref, bf16[2,256,512]{2,1,0:T(8,128)(2,1)} %bitcast.61, bf16[2,256,512]{2,1,0:T(8,128)(2,1)} %bitcast.60, f32[64,64,512]{2,1,0:T(8,128)} %doppler.2.refs_0_, bf16[4,64,128]{2,1,0:T(8,128)(2,1)} %copy-done.9, bf16[4,64,128]{2,1,0:T(8,128)(2,1)} %copy-done.50, ...), custom_call_target="tpu_custom_call" | custom-call | flops 2147483648 | bytes 8388608 | tf_op jit(solution)/shard_map/doppler/pallas_call | solution.py:305
  (281 shorter events, 69.4 us)
Async XLA Ops:
  27.7 52.4 %collective-permute-start = (bf16[2,8,4,64,128]{4,3,2,1,0:T(8,128)(2,1)}, bf16[2,8,4,64,128]{4,3,2,1,0:T(8,128)(2,1)S(1)}, u32[]{:S(2)}, u32[]{:S(2)}) collective-permute-start(bf16[2,8,4,64,128]{4,3,2,1,0:T(8,128)(2,1)} %get-tuple-element.56), channel_id=1, source_target_pairs={{0,8},{8,0},{16,24},{24,16},{1,9},{9,1},{17,25},{25,17},{2,10},{10... | collective-permute-start | bytes 3145736 | tf_op jit(solution)/shard_map/ppermute | solution.py:419
  51.4 26.4 %collective-permute-start.13 = (bf16[2,8,3,64,128]{4,3,2,1,0:T(8,128)(2,1)}, bf16[2,8,3,64,128]{4,3,2,1,0:T(8,128)(2,1)S(1)}, u32[]{:S(2)}, u32[]{:S(2)}) collective-permute-start(bf16[2,8,3,64,128]{4,3,2,1,0:T(8,128)(2,1)} %get-tuple-element.71), channel_id=1, source_target_pairs={{0,16},{8,24},{16,0},{24,8},{1,17},{9,25},{17,1},{25,9},{2,18},{10... | collective-permute-start | bytes 2359304 | tf_op jit(solution)/shard_map/ppermute | solution.py:419
  51.7 40.4 %collective-permute-start.2 = (bf16[2,8,4,64,128]{4,3,2,1,0:T(8,128)(2,1)}, bf16[2,8,4,64,128]{4,3,2,1,0:T(8,128)(2,1)}, u32[]{:S(2)}, u32[]{:S(2)}) collective-permute-start(bf16[2,8,4,64,128]{4,3,2,1,0:T(8,128)(2,1)} %get-tuple-element.58), channel_id=1, source_target_pairs={{0,16},{8,24},{16,0},{24,8},{1,17},{9,25},{17,1},{25,9},{2,18},{10... | collective-permute-start | bytes 3145736 | tf_op jit(solution)/shard_map/ppermute | solution.py:419
  77.3 25.9 %collective-permute-start.35 = (bf16[2,8,2,64,128]{4,3,2,1,0:T(8,128)(2,1)}, bf16[2,8,2,64,128]{4,3,2,1,0:T(8,128)(2,1)S(1)}, u32[]{:S(2)}, u32[]{:S(2)}) collective-permute-start(bf16[2,8,2,64,128]{4,3,2,1,0:T(8,128)(2,1)} %get-tuple-element.97), channel_id=1, source_target_pairs={{0,16},{8,24},{16,0},{24,8},{1,17},{9,25},{17,1},{25,9},{2,18},{10... | collective-permute-start | bytes 1572872 | tf_op jit(solution)/shard_map/ppermute | solution.py:419
  77.6 27.8 %collective-permute-start.33 = (bf16[2,8,2,64,128]{4,3,2,1,0:T(8,128)(2,1)}, bf16[2,8,2,64,128]{4,3,2,1,0:T(8,128)(2,1)S(1)}, u32[]{:S(2)}, u32[]{:S(2)}) collective-permute-start(bf16[2,8,2,64,128]{4,3,2,1,0:T(8,128)(2,1)} %get-tuple-element.95), channel_id=1, source_target_pairs={{0,8},{8,0},{16,24},{24,16},{1,9},{9,1},{17,25},{25,17},{2,10},{10... | collective-permute-start | bytes 1572872 | tf_op jit(solution)/shard_map/ppermute | solution.py:419
  78.9 50.2 %collective-permute-start.14 = (bf16[1,8,3,64,128]{4,3,2,1,0:T(8,128)(2,1)}, bf16[1,8,3,64,128]{4,3,2,1,0:T(8,128)(2,1)}, u32[]{:S(2)}, u32[]{:S(2)}) collective-permute-start(bf16[1,8,3,64,128]{4,3,2,1,0:T(8,128)(2,1)} %get-tuple-element.116), channel_id=1, source_target_pairs={{0,8},{8,0},{16,24},{24,16},{1,9},{9,1},{17,25},{25,17},{2,10},{10... | collective-permute-start | bytes 1179656 | tf_op jit(solution)/shard_map/ppermute | solution.py:419
  80.1 49.5 %collective-permute-start.12 = (bf16[1,8,3,64,128]{4,3,2,1,0:T(8,128)(2,1)}, bf16[1,8,3,64,128]{4,3,2,1,0:T(8,128)(2,1)}, u32[]{:S(2)}, u32[]{:S(2)}) collective-permute-start(bf16[1,8,3,64,128]{4,3,2,1,0:T(8,128)(2,1)} %get-tuple-element.118), channel_id=1, source_target_pairs={{0,16},{8,24},{16,0},{24,8},{1,17},{9,25},{17,1},{25,9},{2,18},{10... | collective-permute-start | bytes 1179656 | tf_op jit(solution)/shard_map/ppermute | solution.py:419
  92.1 30.9 %collective-permute-start.1 = (bf16[1,8,4,64,128]{4,3,2,1,0:T(8,128)(2,1)S(1)}, bf16[1,8,4,64,128]{4,3,2,1,0:T(8,128)(2,1)S(1)}, u32[]{:S(2)}, u32[]{:S(2)}) collective-permute-start(bf16[1,8,4,64,128]{4,3,2,1,0:T(8,128)(2,1)S(1)} %get-tuple-element.110), channel_id=1, source_target_pairs={{0,16},{8,24},{16,0},{24,8},{1,17},{9,25},{17,1},{25,9},{2,18},{10... | collective-permute-start | bytes 1572872 | tf_op jit(solution)/shard_map/ppermute | solution.py:419
  103.2 21.3 %collective-permute-start.3 = (bf16[1,8,4,64,128]{4,3,2,1,0:T(8,128)(2,1)}, bf16[1,8,4,64,128]{4,3,2,1,0:T(8,128)(2,1)S(1)}, u32[]{:S(2)}, u32[]{:S(2)}) collective-permute-start(bf16[1,8,4,64,128]{4,3,2,1,0:T(8,128)(2,1)} %get-tuple-element.108), channel_id=1, source_target_pairs={{0,8},{8,0},{16,24},{24,16},{1,9},{9,1},{17,25},{25,17},{2,10},{10... | collective-permute-start | bytes 1572872 | tf_op jit(solution)/shard_map/ppermute | solution.py:419
  105.3 26.5 %collective-permute-start.36 = (bf16[1,8,2,64,128]{4,3,2,1,0:T(8,128)(2,1)}, bf16[1,8,2,64,128]{4,3,2,1,0:T(8,128)(2,1)}, u32[]{:S(2)}, u32[]{:S(2)}) collective-permute-start(bf16[1,8,2,64,128]{4,3,2,1,0:T(8,128)(2,1)} %get-tuple-element.120), channel_id=1, source_target_pairs={{0,8},{8,0},{16,24},{24,16},{1,9},{9,1},{17,25},{25,17},{2,10},{10... | collective-permute-start | bytes 786440 | tf_op jit(solution)/shard_map/ppermute | solution.py:419
  129.7 19.9 %collective-permute-start.5 = (bf16[9,64,128]{2,1,0:T(8,128)(2,1)S(1)}, bf16[9,64,128]{2,1,0:T(8,128)(2,1)S(1)}, u32[]{:S(2)}, u32[]{:S(2)}) collective-permute-start(bf16[9,64,128]{2,1,0:T(8,128)(2,1)S(1)} %get-tuple-element.62), channel_id=1, source_target_pairs={{0,2},{1,3},{2,0},{3,1},{4,6},{5,7},{6,4},{7,5},{8,10},{9,11},{10,... | collective-permute-start | bytes 442376 | tf_op jit(solution)/shard_map/ppermute | solution.py:465
  131.8 19.0 %collective-permute-start.6 = (bf16[9,64,128]{2,1,0:T(8,128)(2,1)S(1)}, bf16[9,64,128]{2,1,0:T(8,128)(2,1)S(1)}, u32[]{:S(2)}, u32[]{:S(2)}) collective-permute-start(bf16[9,64,128]{2,1,0:T(8,128)(2,1)S(1)} %get-tuple-element.63), channel_id=1, source_target_pairs={{0,3},{1,2},{2,1},{3,0},{4,7},{5,6},{6,5},{7,4},{8,11},{9,10},{10,... | collective-permute-start | bytes 442376 | tf_op jit(solution)/shard_map/ppermute | solution.py:465
  132.3 19.8 %collective-permute-start.7 = (bf16[9,64,128]{2,1,0:T(8,128)(2,1)S(1)}, bf16[9,64,128]{2,1,0:T(8,128)(2,1)S(1)}, u32[]{:S(2)}, u32[]{:S(2)}) collective-permute-start(bf16[9,64,128]{2,1,0:T(8,128)(2,1)S(1)} %get-tuple-element.64), channel_id=1, source_target_pairs={{0,4},{1,5},{2,6},{3,7},{4,0},{5,1},{6,2},{7,3},{8,12},{9,13},{10,... | collective-permute-start | bytes 442376 | tf_op jit(solution)/shard_map/ppermute | solution.py:465
  136.9 19.8 %collective-permute-start.9 = (bf16[9,64,128]{2,1,0:T(8,128)(2,1)S(1)}, bf16[9,64,128]{2,1,0:T(8,128)(2,1)S(1)}, u32[]{:S(2)}, u32[]{:S(2)}) collective-permute-start(bf16[9,64,128]{2,1,0:T(8,128)(2,1)S(1)} %get-tuple-element.66), channel_id=1, source_target_pairs={{0,6},{1,7},{2,4},{3,5},{4,2},{5,3},{6,0},{7,1},{8,14},{9,15},{10,... | collective-permute-start | bytes 442376 | tf_op jit(solution)/shard_map/ppermute | solution.py:465
  149.6 18.5 %collective-permute-start.24 = (bf16[2,8,3,64,128]{4,3,2,1,0:T(8,128)(2,1)}, bf16[2,8,3,64,128]{4,3,2,1,0:T(8,128)(2,1)}, u32[]{:S(2)}, u32[]{:S(2)}) collective-permute-start(bf16[2,8,3,64,128]{4,3,2,1,0:T(8,128)(2,1)} %get-tuple-element.84), channel_id=1, source_target_pairs={{0,16},{8,24},{16,0},{24,8},{1,17},{9,25},{17,1},{25,9},{2,18},{10... | collective-permute-start | bytes 2359304 | tf_op jit(solution)/shard_map/ppermute | solution.py:419
  150.9 20.0 %collective-permute-start.22 = (bf16[2,8,3,64,128]{4,3,2,1,0:T(8,128)(2,1)}, bf16[2,8,3,64,128]{4,3,2,1,0:T(8,128)(2,1)}, u32[]{:S(2)}, u32[]{:S(2)}) collective-permute-start(bf16[2,8,3,64,128]{4,3,2,1,0:T(8,128)(2,1)} %get-tuple-element.82), channel_id=1, source_target_pairs={{0,8},{8,0},{16,24},{24,16},{1,9},{9,1},{17,25},{25,17},{2,10},{10... | collective-permute-start | bytes 2359304 | tf_op jit(solution)/shard_map/ppermute | solution.py:419
  152.1 24.5 %collective-permute-start.15 = (bf16[6,64,128]{2,1,0:T(8,128)(2,1)}, bf16[6,64,128]{2,1,0:T(8,128)(2,1)}, u32[]{:S(2)}, u32[]{:S(2)}) collective-permute-start(bf16[6,64,128]{2,1,0:T(8,128)(2,1)} %get-tuple-element.74), channel_id=1, source_target_pairs={{0,1},{1,0},{2,3},{3,2},{4,5},{5,4},{6,7},{7,6},{8,9},{9,8},{10,11... | collective-permute-start | bytes 294920 | tf_op jit(solution)/shard_map/ppermute | solution.py:465
  154.0 34.6 %collective-permute-start.16 = (bf16[6,64,128]{2,1,0:T(8,128)(2,1)}, bf16[6,64,128]{2,1,0:T(8,128)(2,1)}, u32[]{:S(2)}, u32[]{:S(2)}) collective-permute-start(bf16[6,64,128]{2,1,0:T(8,128)(2,1)} %get-tuple-element.75), channel_id=1, source_target_pairs={{0,2},{1,3},{2,0},{3,1},{4,6},{5,7},{6,4},{7,5},{8,10},{9,11},{10,... | collective-permute-start | bytes 294920 | tf_op jit(solution)/shard_map/ppermute | solution.py:465
  156.8 33.4 %collective-permute-start.17 = (bf16[6,64,128]{2,1,0:T(8,128)(2,1)}, bf16[6,64,128]{2,1,0:T(8,128)(2,1)}, u32[]{:S(2)}, u32[]{:S(2)}) collective-permute-start(bf16[6,64,128]{2,1,0:T(8,128)(2,1)} %get-tuple-element.76), channel_id=1, source_target_pairs={{0,3},{1,2},{2,1},{3,0},{4,7},{5,6},{6,5},{7,4},{8,11},{9,10},{10,... | collective-permute-start | bytes 294920 | tf_op jit(solution)/shard_map/ppermute | solution.py:465
  203.5 23.4 %collective-permute-start.32 = (bf16[6,64,128]{2,1,0:T(8,128)(2,1)S(1)}, bf16[6,64,128]{2,1,0:T(8,128)(2,1)S(1)}, u32[]{:S(2)}, u32[]{:S(2)}) collective-permute-start(bf16[6,64,128]{2,1,0:T(8,128)(2,1)S(1)} %get-tuple-element.93), channel_id=1, source_target_pairs={{0,7},{1,6},{2,5},{3,4},{4,3},{5,2},{6,1},{7,0},{8,15},{9,14},{10,... | collective-permute-start | bytes 294920 | tf_op jit(solution)/shard_map/ppermute | solution.py:465
  207.2 31.9 %collective-permute-start.39 = (bf16[4,64,128]{2,1,0:T(8,128)(2,1)S(1)}, bf16[4,64,128]{2,1,0:T(8,128)(2,1)S(1)}, u32[]{:S(2)}, u32[]{:S(2)}) collective-permute-start(bf16[4,64,128]{2,1,0:T(8,128)(2,1)S(1)} %copy-done.32), channel_id=1, source_target_pairs={{0,3},{1,2},{2,1},{3,0},{4,7},{5,6},{6,5},{7,4},{8,11},{9,10},{10,... | collective-permute-start | bytes 196616 | tf_op jit(solution)/shard_map/ppermute | solution.py:465
  209.2 30.0 %collective-permute-start.40 = (bf16[4,64,128]{2,1,0:T(8,128)(2,1)S(1)}, bf16[4,64,128]{2,1,0:T(8,128)(2,1)S(1)}, u32[]{:S(2)}, u32[]{:S(2)}) collective-permute-start(bf16[4,64,128]{2,1,0:T(8,128)(2,1)S(1)} %copy-done.30), channel_id=1, source_target_pairs={{0,4},{1,5},{2,6},{3,7},{4,0},{5,1},{6,2},{7,3},{8,12},{9,13},{10,... | collective-permute-start | bytes 196616 | tf_op jit(solution)/shard_map/ppermute | solution.py:465
  214.6 24.5 %collective-permute-start.41 = (bf16[4,64,128]{2,1,0:T(8,128)(2,1)S(1)}, bf16[4,64,128]{2,1,0:T(8,128)(2,1)S(1)}, u32[]{:S(2)}, u32[]{:S(2)}) collective-permute-start(bf16[4,64,128]{2,1,0:T(8,128)(2,1)S(1)} %copy-done.28), channel_id=1, source_target_pairs={{0,5},{1,4},{2,7},{3,6},{4,1},{5,0},{6,3},{7,2},{8,13},{9,12},{10,... | collective-permute-start | bytes 196616 | tf_op jit(solution)/shard_map/ppermute | solution.py:465
  218.5 20.7 %collective-permute-start.42 = (bf16[4,64,128]{2,1,0:T(8,128)(2,1)S(1)}, bf16[4,64,128]{2,1,0:T(8,128)(2,1)S(1)}, u32[]{:S(2)}, u32[]{:S(2)}) collective-permute-start(bf16[4,64,128]{2,1,0:T(8,128)(2,1)S(1)} %copy-done.26), channel_id=1, source_target_pairs={{0,6},{1,7},{2,4},{3,5},{4,2},{5,3},{6,0},{7,1},{8,14},{9,15},{10,... | collective-permute-start | bytes 196616 | tf_op jit(solution)/shard_map/ppermute | solution.py:465
  (89 other events, 1034.2 us)
